TPU v7x, 32 devices: a whole 2x2x4 slice. The times are simulated.
32 devices in a mesh: row: 16 (over z, y, core), col: 2 (over x).
Axes of the slice: x: 2, y: 2, z: 4, core: 2. Of those that a mesh axis runs over, the one named last changes fastest.
Arguments:
- tokens: bfloat16 [16384, 512], P('row', 'col'), may hold values from -6 to 6
- prev_logits: bfloat16 [16, 8, 1024, 1024], P('row', 'col'), may hold values from -9 to 9
- qkv_weight: bfloat16 [512, 1536], P('row', 'col'), may hold values from -0.25 to 0.25
- qkv_bias: bfloat16 [1536], P('col'), may hold values from -2 to 2
- out_weight: bfloat16 [512, 512], P('col', 'row'), may hold values from -1 to 1
- out_bias: bfloat16 [512], P('col'), may hold values from -1.5 to 1.5
- norm1_gain: bfloat16 [512], P('col'), may hold values from 0.25 to 1.75
- norm1_shift: bfloat16 [512], P('col'), may hold values from -2 to 2
- ff1_weight: bfloat16 [512, 2048], P('row', 'col'), may hold values from -0.25 to 0.25
- ff1_bias: bfloat16 [2048], P('col'), may hold values from -2 to 2
- ff2_weight: bfloat16 [2048, 512], P('col', 'row'), may hold values from -0.125 to 0.125
- ff2_bias: bfloat16 [512], P('col'), may hold values from -1.5 to 1.5
- norm2_gain: bfloat16 [512], P('col'), may hold values from 0.25 to 1.75
- norm2_shift: bfloat16 [512], P('col'), may hold values from -2 to 2
- out_grad: bfloat16 [16384, 512], P('row', 'col'), may hold values from -6 to 6
- logit_grad: bfloat16 [16, 8, 1024, 1024], P('row', 'col'), may hold values from -0.3984375 to 0.3984375
Outputs:
- output: bfloat16 [16384, 512], P('row', 'col')
- raw_logits: bfloat16 [16, 8, 1024, 1024], P('row', 'col')
- input_grad: bfloat16 [16384, 512], P('row', 'col')
- prev_grad: bfloat16 [16, 8, 1024, 1024], P('row', 'col')
- qkv_weight_grad: float32 [512, 1536], P('row', 'col')
- qkv_bias_grad: float32 [1536], P('col')
- out_weight_grad: float32 [512, 512], P('col', 'row')
- out_bias_grad: float32 [512], P('col')
- norm1_gain_grad: float32 [512], P('col')
- norm1_shift_grad: float32 [512], P('col')
- ff1_weight_grad: float32 [512, 2048], P('row', 'col')
- ff1_bias_grad: float32 [2048], P('col')
- ff2_weight_grad: float32 [2048, 512], P('col', 'row')
- ff2_bias_grad: float32 [512], P('col')
- norm2_gain_grad: float32 [512], P('col')
- norm2_shift_grad: float32 [512], P('col')
All inputs are finite; a program needn't handle non-finite values.
Results may differ from a plain program's by a relative error of at most 0.011.
Values may be sent and summed in bfloat16 or wider, within the bound.
A program may use at most 128 MiB of HBM per device.

v0:
```python
import math

import jax
import jax.numpy as jnp
from jax import lax
from jax.sharding import PartitionSpec as P

D = 512
DH = 64


norm_eps = 1e-06
root_half = 0.7071067811865476
inv_root_two_pi = 0.3989422804014327


def gelu_value(inner):
    return inner * 0.5 * (1.0 + lax.erf(inner * root_half))


def gelu_slope(inner):
    return 0.5 * (1.0 + lax.erf(inner * root_half)) + inner * inv_root_two_pi * jnp.exp(
        -0.5 * inner * inner
    )


def widen(shard):
    return lax.all_gather(shard, "col", axis=1, tiled=True)


def settle(partial_value):
    return lax.psum_scatter(partial_value, "col", scatter_dimension=1, tiled=True)


def row_totals(first, second):
    return lax.psum((jnp.sum(first, axis=1), jnp.sum(second, axis=1)), "col")


def norm_forward(hidden, gain, shift):
    row_sum, square_sum = row_totals(hidden, hidden * hidden)
    mean_value = row_sum / D
    variance = square_sum / D - mean_value * mean_value
    inv_std = lax.rsqrt(variance + norm_eps)
    centered = (hidden - mean_value[:, None]) * inv_std[:, None]
    return (centered * gain.astype(jnp.float32) + shift.astype(jnp.float32), centered, inv_std)


def norm_backward(grad_out, centered, inv_std, gain):
    scaled = grad_out * gain.astype(jnp.float32)
    grad_sum, cross_sum = row_totals(scaled, scaled * centered)
    grad_in = inv_std[:, None] * (
        scaled - grad_sum[:, None] / D - centered * (cross_sum[:, None] / D)
    )
    return (grad_in, jnp.sum(grad_out * centered, axis=0), jnp.sum(grad_out, axis=0))


def attend_forward(queries, keys_all, values_all, previous, block_rows):
    group_count, seq_len, head_width = queries.shape
    block_count = seq_len // block_rows
    score_scale = 1.0 / math.sqrt(head_width)

    def one_group(operands):
        query_group, key_group, value_group, prev_group = operands

        def one_block(pieces):
            query_block, prev_block = pieces
            scores = (
                prev_block.astype(jnp.float32)
                + jnp.einsum(
                    "qe,ke->qk", query_block, key_group, preferred_element_type=jnp.float32
                )
                * score_scale
            )
            top_score = jnp.max(scores, axis=1, keepdims=True)
            exponent = jnp.exp(scores - top_score)
            row_total = jnp.sum(exponent, axis=1, keepdims=True)
            probs_low = (exponent / row_total).astype(jnp.bfloat16)
            attended = jnp.dot(probs_low, value_group, preferred_element_type=jnp.float32)
            return (attended, scores.astype(jnp.bfloat16), (top_score + jnp.log(row_total))[:, 0])

        return lax.map(
            one_block,
            (
                query_group.reshape(block_count, block_rows, head_width),
                prev_group.reshape(block_count, block_rows, seq_len),
            ),
        )

    attended, raw_scores, log_totals = lax.map(one_group, (queries, keys_all, values_all, previous))
    return (
        attended.reshape(group_count, seq_len, head_width),
        raw_scores.reshape(group_count, seq_len, seq_len),
        log_totals.reshape(group_count, seq_len),
    )


def attend_backward(
    queries, keys_all, values_all, previous, log_totals, attended_grad, score_cotangent, block_rows
):
    group_count, seq_len, head_width = queries.shape
    block_count = seq_len // block_rows
    score_scale = 1.0 / math.sqrt(head_width)

    def one_group(operands):
        query_group, key_group, value_group, prev_group, log_group, grad_group, cotangent_group = (
            operands
        )

        def one_block(accums, pieces):
            key_grad, value_grad = accums
            query_block, prev_block, log_block, grad_block, cotangent_block = pieces
            scores = (
                prev_block.astype(jnp.float32)
                + jnp.einsum(
                    "qe,ke->qk", query_block, key_group, preferred_element_type=jnp.float32
                )
                * score_scale
            )
            probs = jnp.exp(scores - log_block[:, None])
            probs_low = probs.astype(jnp.bfloat16)
            probs_grad = jnp.einsum(
                "qe,ke->qk", grad_block, value_group, preferred_element_type=jnp.float32
            )
            row_delta = jnp.sum(probs_grad * probs, axis=1, keepdims=True)
            score_grad = (
                probs * (probs_grad - row_delta) + cotangent_block.astype(jnp.float32)
            ).astype(jnp.bfloat16)
            query_grad = (
                jnp.dot(score_grad, key_group, preferred_element_type=jnp.float32) * score_scale
            )
            key_grad = (
                key_grad
                + jnp.einsum(
                    "qk,qe->ke", score_grad, query_block, preferred_element_type=jnp.float32
                )
                * score_scale
            )
            value_grad = value_grad + jnp.einsum(
                "qk,qe->ke", probs_low, grad_block, preferred_element_type=jnp.float32
            )
            return ((key_grad, value_grad), (query_grad, score_grad))

        zero_keys = jnp.zeros((seq_len, head_width), jnp.float32)
        (key_grad, value_grad), (query_grad, score_grad) = lax.scan(
            one_block,
            (zero_keys, zero_keys),
            (
                query_group.reshape(block_count, block_rows, head_width),
                prev_group.reshape(block_count, block_rows, seq_len),
                log_group.reshape(block_count, block_rows),
                grad_group.reshape(block_count, block_rows, head_width),
                cotangent_group.reshape(block_count, block_rows, seq_len),
            ),
        )
        return (
            query_grad.reshape(seq_len, head_width),
            key_grad,
            value_grad,
            score_grad.reshape(seq_len, seq_len),
        )

    return lax.map(
        one_group,
        (queries, keys_all, values_all, previous, log_totals, attended_grad, score_cotangent),
    )


def per_device(
    tokens,
    prev_logits,
    qkv_weight,
    qkv_bias,
    out_weight,
    out_bias,
    norm1_gain,
    norm1_shift,
    ff1_weight,
    ff1_bias,
    ff2_weight,
    ff2_bias,
    norm2_gain,
    norm2_shift,
    out_grad,
    logit_grad,
):
    wide_qkv, wide_out, wide_ff1, wide_ff2 = (
        lax.all_gather(qkv_weight, "row", axis=0, tiled=True),
        lax.all_gather(out_weight, "row", axis=1, tiled=True),
        lax.all_gather(ff1_weight, "row", axis=0, tiled=True),
        lax.all_gather(ff2_weight, "row", axis=1, tiled=True),
    )
    seq_count = prev_logits.shape[0]
    head_count = prev_logits.shape[1]
    seq_len = prev_logits.shape[2]
    row_count = tokens.shape[0]
    group_count = seq_count * head_count
    block_rows = min(512, seq_len)
    tokens_full = widen(tokens)
    projected = (
        jnp.dot(tokens_full, wide_qkv, preferred_element_type=jnp.float32)
        + qkv_bias.astype(jnp.float32)
    ).astype(jnp.bfloat16)
    by_head = (
        projected.reshape(seq_count, seq_len, head_count, 3, DH)
        .transpose(3, 0, 2, 1, 4)
        .reshape(3, group_count, seq_len, DH)
    )
    prev_groups = prev_logits.reshape(group_count, seq_len, seq_len)
    attended, raw_scores, log_totals = attend_forward(
        by_head[0], by_head[1], by_head[2], prev_groups, block_rows
    )
    merged = (
        attended.astype(jnp.bfloat16)
        .reshape(seq_count, head_count, seq_len, DH)
        .transpose(0, 2, 1, 3)
        .reshape(row_count, head_count * DH)
    )
    branch_one = settle(jnp.dot(merged, wide_out, preferred_element_type=jnp.float32))
    branch_one = branch_one + out_bias.astype(jnp.float32)
    normed_one, centered_one, inv_one = norm_forward(
        tokens.astype(jnp.float32) + branch_one, norm1_gain, norm1_shift
    )
    normed_low = normed_one.astype(jnp.bfloat16)
    ffn_input = widen(normed_low)
    inner = jnp.dot(ffn_input, wide_ff1, preferred_element_type=jnp.float32) + ff1_bias.astype(
        jnp.float32
    )
    activated = gelu_value(inner).astype(jnp.bfloat16)
    branch_two = settle(jnp.dot(activated, wide_ff2, preferred_element_type=jnp.float32))
    branch_two = branch_two + ff2_bias.astype(jnp.float32)
    normed_two, centered_two, inv_two = norm_forward(
        normed_one + branch_two, norm2_gain, norm2_shift
    )
    output = normed_two.astype(jnp.bfloat16)
    grad_two, gain_two_grad, shift_two_grad = norm_backward(
        out_grad.astype(jnp.float32), centered_two, inv_two, norm2_gain
    )
    branch_two_grad = grad_two.astype(jnp.bfloat16)
    ff2_bias_grad = jnp.sum(branch_two_grad.astype(jnp.float32), axis=0)
    grad_rows_in = widen(branch_two_grad)
    inner_grad = (
        jnp.einsum("rd,fd->rf", grad_rows_in, wide_ff2, preferred_element_type=jnp.float32)
        * gelu_slope(inner)
    ).astype(jnp.bfloat16)
    normed_grad_part = settle(
        jnp.einsum("rf,df->rd", inner_grad, wide_ff1, preferred_element_type=jnp.float32)
    )
    ff1_grad_wide = jnp.einsum(
        "rd,rf->df", ffn_input, inner_grad, preferred_element_type=jnp.float32
    )
    ff2_grad_wide = jnp.einsum(
        "rf,rd->fd", activated, grad_rows_in, preferred_element_type=jnp.float32
    )
    ff1_bias_grad = jnp.sum(inner_grad.astype(jnp.float32), axis=0)
    grad_one, gain_one_grad, shift_one_grad = norm_backward(
        grad_two + normed_grad_part, centered_one, inv_one, norm1_gain
    )
    branch_one_grad = grad_one.astype(jnp.bfloat16)
    out_bias_grad = jnp.sum(branch_one_grad.astype(jnp.float32), axis=0)
    branch_grad_full = widen(branch_one_grad)
    merged_grad = jnp.einsum(
        "rd,hd->rh", branch_grad_full, wide_out, preferred_element_type=jnp.float32
    ).astype(jnp.bfloat16)
    out_grad_wide = jnp.einsum(
        "rh,rd->hd", merged, branch_grad_full, preferred_element_type=jnp.float32
    )
    attended_grad = (
        merged_grad.reshape(seq_count, seq_len, head_count, DH)
        .transpose(0, 2, 1, 3)
        .reshape(group_count, seq_len, DH)
    )
    query_grad, key_grad, value_grad, score_grad = attend_backward(
        by_head[0],
        by_head[1],
        by_head[2],
        prev_groups,
        log_totals,
        attended_grad,
        logit_grad.reshape(group_count, seq_len, seq_len),
        block_rows,
    )
    projected_grad = (
        jnp.stack((query_grad, key_grad, value_grad), axis=0)
        .astype(jnp.bfloat16)
        .reshape(3, seq_count, head_count, seq_len, DH)
        .transpose(1, 3, 2, 0, 4)
        .reshape(row_count, 3 * head_count * DH)
    )
    qkv_bias_grad = jnp.sum(projected_grad.astype(jnp.float32), axis=0)
    input_part = settle(
        jnp.einsum("rc,dc->rd", projected_grad, wide_qkv, preferred_element_type=jnp.float32)
    )
    input_grad = (grad_one + input_part).astype(jnp.bfloat16)
    qkv_grad_wide = jnp.einsum(
        "rd,rc->dc", tokens_full, projected_grad, preferred_element_type=jnp.float32
    )
    weight_grads = (
        lax.psum_scatter(qkv_grad_wide, "row", scatter_dimension=0, tiled=True),
        lax.psum_scatter(out_grad_wide, "row", scatter_dimension=1, tiled=True),
        lax.psum_scatter(ff1_grad_wide, "row", scatter_dimension=0, tiled=True),
        lax.psum_scatter(ff2_grad_wide, "row", scatter_dimension=1, tiled=True),
    )
    vector_grads = lax.psum(
        (
            qkv_bias_grad,
            out_bias_grad,
            gain_one_grad,
            shift_one_grad,
            ff1_bias_grad,
            ff2_bias_grad,
            gain_two_grad,
            shift_two_grad,
        ),
        "row",
    )
    return (
        output,
        raw_scores.reshape(prev_logits.shape),
        input_grad,
        score_grad.reshape(prev_logits.shape),
        weight_grads[0],
        vector_grads[0],
        weight_grads[1],
        vector_grads[1],
        vector_grads[2],
        vector_grads[3],
        weight_grads[2],
        vector_grads[4],
        weight_grads[3],
        vector_grads[5],
        vector_grads[6],
        vector_grads[7],
    )


def solution(mesh):
    in_specs = (
        P("row", "col"),
        P("row", "col", None, None),
        P("row", "col"),
        P("col"),
        P("col", "row"),
        P("col"),
        P("col"),
        P("col"),
        P("row", "col"),
        P("col"),
        P("col", "row"),
        P("col"),
        P("col"),
        P("col"),
        P("row", "col"),
        P("row", "col", None, None),
    )
    out_specs = (
        P("row", "col"),
        P("row", "col", None, None),
        P("row", "col"),
        P("row", "col", None, None),
        P("row", "col"),
        P("col"),
        P("col", "row"),
        P("col"),
        P("col"),
        P("col"),
        P("row", "col"),
        P("col"),
        P("col", "row"),
        P("col"),
        P("col"),
        P("col"),
    )
    return jax.shard_map(
        per_device, mesh=mesh, in_specs=in_specs, out_specs=out_specs, check_vma=False
    )
```

profile of v0, /device:TPU:0, one launch (start us, length us, event | category | flops | bytes accessed | tf_op | source)
XLA Modules:
  0.0 793.2 jit_solution(15190332763168429825)
XLA Ops:
  9.5 24.1 %all_gather.26 = bf16[256,512]{0,1:T(8,128)(2,1)S(1)} all-gather(bf16[256,32]{0,1:T(8,128)(2,1)} %param.28), channel_id=1, replica_groups=mesh['row'=16,'col'=2] {'row'}, dimensions={1}, use_global_device_ids=true | all-gather | bytes 278528 | tf_op jit(solution)/shard_map/all_gather | solution.py:188
  33.6 19.8 %all_gather.25 = bf16[512,768]{1,0:T(8,128)(2,1)S(1)} all-gather(bf16[32,768]{1,0:T(8,128)(2,1)} %param.26), channel_id=1, replica_groups=mesh['row'=16,'col'=2] {'row'}, dimensions={0}, use_global_device_ids=true | all-gather | bytes 835584 | tf_op jit(solution)/shard_map/all_gather | solution.py:187
  53.4 3.7 add_convert_fusion
  61.9 78.9 %while.62 = (s32[]{:T(128)}, bf16[4,2,512,64]{2,3,1,0:T(8,128)(2,1)}, bf16[4,2,512,1024]{3,2,1,0:T(8,128)(2,1)}, f32[4,2,512]{2,1,0:T(2,128)S(1)}, bf16[4,1024,6...) while((s32[]{:T(128)}, ...), condition=%wide.region_5.6_spmd, body=%wide.region_0.5_spmd.sunk | while | flops 139460096 | bytes 37516700 | solution.py:89
  64.0 3.1 constant_dynamic-slice_fusion.14
  67.1 10.8 %while.65 = (s32[]{:T(128)}, bf16[2,512,64]{1,2,0:T(8,128)(2,1)S(1)}, bf16[2,512,1024]{2,1,0:T(8,128)(2,1)}, f32[2,512]{1,0:T(2,128)S(1)}, bf16[2,512,1024]{2,1,...) while((s32[]{:T(128)}, ...), condition=%wide.region_4.4_spmd, body=%wide.region_1.3_spmd.sunk | while | flops 139460096 | bytes 28071088 | solution.py:81
  78.5 3.1 bitcast_dynamic-update-slice_fusion.16
  83.7 3.1 constant_dynamic-slice_fusion.14
  86.8 10.8 %while.65 = (s32[]{:T(128)}, bf16[2,512,64]{1,2,0:T(8,128)(2,1)S(1)}, bf16[2,512,1024]{2,1,0:T(8,128)(2,1)}, f32[2,512]{1,0:T(2,128)S(1)}, bf16[2,512,1024]{2,1,...) while((s32[]{:T(128)}, ...), condition=%wide.region_4.4_spmd, body=%wide.region_1.3_spmd.sunk | while | flops 139460096 | bytes 28071088 | solution.py:81
  98.3 3.1 bitcast_dynamic-update-slice_fusion.16
  103.4 3.1 constant_dynamic-slice_fusion.14
  106.5 10.8 %while.65 = (s32[]{:T(128)}, bf16[2,512,64]{1,2,0:T(8,128)(2,1)S(1)}, bf16[2,512,1024]{2,1,0:T(8,128)(2,1)}, f32[2,512]{1,0:T(2,128)S(1)}, bf16[2,512,1024]{2,1,...) while((s32[]{:T(128)}, ...), condition=%wide.region_4.4_spmd, body=%wide.region_1.3_spmd.sunk | while | flops 139460096 | bytes 28071088 | solution.py:81
  123.1 3.1 constant_dynamic-slice_fusion.14
  126.2 10.8 %while.65 = (s32[]{:T(128)}, bf16[2,512,64]{1,2,0:T(8,128)(2,1)S(1)}, bf16[2,512,1024]{2,1,0:T(8,128)(2,1)}, f32[2,512]{1,0:T(2,128)S(1)}, bf16[2,512,1024]{2,1,...) while((s32[]{:T(128)}, ...), condition=%wide.region_4.4_spmd, body=%wide.region_1.3_spmd.sunk | while | flops 139460096 | bytes 28071088 | solution.py:81
  137.7 3.1 bitcast_dynamic-update-slice_fusion.16
  145.3 29.8 %reduce-scatter.11.cloned.1.call-done = f32[1024,256]{1,0:T(8,128)} async-done(((f32[1024,512]{1,0:T(8,128)}), f32[1024,256]{1,0:T(8,128)}) %reduce-scatter.11.cloned.1.call-update) | async-done | bytes 1048592 | tf_op jit(solution)/shard_map/reduce_scatter | solution.py:32
  176.7 5.0 all-reduce.4
  183.5 22.1 %all-gather.9.cloned.1.call-done = bf16[1024,512]{1,0:T(8,128)(2,1)} async-done(((bf16[1024,256]{1,0:T(8,128)(2,1)}), bf16[1024,512]{1,0:T(8,128)(2,1)}) %all-gather.9.cloned.1.call-update) | async-done | bytes 1048592 | tf_op jit(solution)/shard_map/all_gather | solution.py:28
  205.6 5.7 multiply_convert_fusion
  211.4 34.2 %all-gather.13.cloned.1.call-done = bf16[1024,512]{0,1:T(8,128)(2,1)} async-done(((bf16[1024,32]{0,1:T(8,128)(2,1)}), bf16[1024,512]{0,1:T(8,128)(2,1)}) %all-gather.13.cloned.1.call-update) | async-done | bytes 1048592 | tf_op jit(solution)/shard_map/all_gather | solution.py:190
  245.6 4.4 fusion.47
  250.7 30.3 %reduce-scatter.13.cloned.1.call-done = f32[1024,256]{1,0:T(8,128)} async-done(((f32[1024,512]{1,0:T(8,128)}), f32[1024,256]{1,0:T(8,128)}) %reduce-scatter.13.cloned.1.call-update) | async-done | bytes 1048592 | tf_op jit(solution)/shard_map/reduce_scatter | solution.py:32
  282.9 5.0 all-reduce.3
  289.0 5.0 all-reduce.2
  296.3 21.2 %all-gather.15.cloned.1.call-done = bf16[1024,512]{1,0:T(8,128)(2,1)} async-done(((bf16[1024,256]{1,0:T(8,128)(2,1)}), bf16[1024,512]{1,0:T(8,128)(2,1)}) %all-gather.15.cloned.1.call-update) | async-done | bytes 1048592 | tf_op jit(solution)/shard_map/all_gather | solution.py:28
  317.5 5.5 convert_reduce_fusion
  327.6 31.4 %reduce-scatter.15.cloned.1.call-done = f32[1024,256]{1,0:T(8,128)} async-done(((f32[1024,512]{1,0:T(8,128)}), f32[1024,256]{1,0:T(8,128)}) %reduce-scatter.15.cloned.1.call-update) | async-done | bytes 1048592 | tf_op jit(solution)/shard_map/reduce_scatter | solution.py:32
  359.0 3.8 multiply_reduce_fusion.1
  362.8 5.0 all-reduce.1
  367.8 3.3 convert_reduce_fusion.4
  371.8 20.5 %all-gather.17.cloned.1.call-done = bf16[1024,512]{1,0:T(8,128)(2,1)} async-done(((bf16[1024,256]{1,0:T(8,128)(2,1)}), bf16[1024,512]{1,0:T(8,128)(2,1)}) %all-gather.17.cloned.1.call-update) | async-done | bytes 1048592 | tf_op jit(solution)/shard_map/all_gather | solution.py:28
  395.3 100.1 %while.64 = (s32[]{:T(128)}, bf16[4,1024,64]{1,2,0:T(8,128)(2,1)}, bf16[4,1024,64]{1,2,0:T(8,128)(2,1)}, bf16[4,1024,64]{1,2,0:T(8,128)(2,1)}, bf16[4,1024,1024]...) while((s32[]{:T(128)}, bf16[4,1024,64]{1,2,0:T(8,128)(2,1)}, ...), condition=%wide.region_29.30_spmd, body=%wide.region_25.29_spmd.sunk | while | flops 342195712 | bytes 72511112 | solution.py:162
  400.0 3.1 constant_dynamic-slice_fusion.19
  404.9 11.3 %while.66 = (s32[]{:T(128)}, f32[1024,64]{0,1:T(8,128)}, f32[1024,64]{0,1:T(8,128)S(1)}, bf16[2,512,64]{1,2,0:T(8,128)(2,1)S(1)}, bf16[2,512,1024]{2,1,0:T(8,128...) while((s32[]{:T(128)}, f32[1024,64]{0,1:T(8,128)}, ...), condition=%wide.region_28.28_spmd.clone, body=%wide.region_26.27_spmd.clone.sunk | while | flops 342195712 | bytes 48639288 | solution.py:144
  425.0 3.1 constant_dynamic-slice_fusion.19
  429.9 11.3 %while.66 = (s32[]{:T(128)}, f32[1024,64]{0,1:T(8,128)}, f32[1024,64]{0,1:T(8,128)S(1)}, bf16[2,512,64]{1,2,0:T(8,128)(2,1)S(1)}, bf16[2,512,1024]{2,1,0:T(8,128...) while((s32[]{:T(128)}, f32[1024,64]{0,1:T(8,128)}, ...), condition=%wide.region_28.28_spmd.clone, body=%wide.region_26.27_spmd.clone.sunk | while | flops 342195712 | bytes 48639288 | solution.py:144
  450.1 3.1 constant_dynamic-slice_fusion.19
  454.9 11.3 %while.66 = (s32[]{:T(128)}, f32[1024,64]{0,1:T(8,128)}, f32[1024,64]{0,1:T(8,128)S(1)}, bf16[2,512,64]{1,2,0:T(8,128)(2,1)S(1)}, bf16[2,512,1024]{2,1,0:T(8,128...) while((s32[]{:T(128)}, f32[1024,64]{0,1:T(8,128)}, ...), condition=%wide.region_28.28_spmd.clone, body=%wide.region_26.27_spmd.clone.sunk | while | flops 342195712 | bytes 48639288 | solution.py:144
  475.1 3.1 constant_dynamic-slice_fusion.19
  480.0 11.3 %while.66 = (s32[]{:T(128)}, f32[1024,64]{0,1:T(8,128)}, f32[1024,64]{0,1:T(8,128)S(1)}, bf16[2,512,64]{1,2,0:T(8,128)(2,1)S(1)}, bf16[2,512,1024]{2,1,0:T(8,128...) while((s32[]{:T(128)}, f32[1024,64]{0,1:T(8,128)}, ...), condition=%wide.region_28.28_spmd.clone, body=%wide.region_26.27_spmd.clone.sunk | while | flops 342195712 | bytes 48639288 | solution.py:144
  501.9 4.3 fusion.52
  513.7 3.4 convolution_bitcast_fusion.1
  517.2 3.1 copy.55
  520.4 61.0 %all-reduce = (f32[768]{0:T(1024)}, f32[256]{0:T(256)}, f32[256]{0:T(256)}, f32[256]{0:T(256)}, f32[1024]{0:T(1024)}, /*index=5*/f32[256]{0:T(256)}, f32[256]{0:T(256)}, f32[256]{0:T(256)}) all-reduce(f32[768]{0:T(1024)S(1)} %reduce_sum.173, f32[256]{0:T(256)S(1)} %copy-done.24, ...), channel_id=1, replica_groups=mesh['row'=16,'col'=2] {'row'}, use_global_device_ids=true, to_apply=%region_33.34 | all-reduce | flops 3328 | bytes 26624 | tf_op jit(solution)/shard_map/psum | solution.py:303
  583.6 15.5 %reduce-scatter.23.cloned.1.call-done = f32[1024,32]{0,1:T(8,128)} async-done(((f32[1024,512]{0,1:T(8,128)}), f32[1024,32]{0,1:T(8,128)}) %reduce-scatter.23.cloned.1.call-update) | async-done | bytes 131088 | tf_op jit(solution)/shard_map/reduce_scatter | solution.py:301
  599.0 64.9 %reduce-scatter.21.cloned.1.call-done = f32[32,1024]{1,0:T(8,128)} async-done(((f32[512,1024]{1,0:T(8,128)}), f32[32,1024]{1,0:T(8,128)}) %reduce-scatter.21.cloned.1.call-update) | async-done | bytes 131088 | tf_op jit(solution)/shard_map/reduce_scatter | solution.py:300
  663.9 59.2 %reduce-scatter.19.cloned.1.call-done = f32[256,32]{0,1:T(8,128)} async-done(((f32[256,512]{0,1:T(8,128)}), f32[256,32]{0,1:T(8,128)}) %reduce-scatter.19.cloned.1.call-update) | async-done | bytes 32784 | tf_op jit(solution)/shard_map/reduce_scatter | solution.py:299
  723.2 62.9 %reduce-scatter.25.cloned.1.call-done = f32[32,768]{1,0:T(8,128)} async-done(((f32[512,768]{1,0:T(8,128)}), f32[32,768]{1,0:T(8,128)}) %reduce-scatter.25.cloned.1.call-update) | async-done | bytes 98320
  (446 shorter events, 188.2 us)
Async XLA Ops:
  8.0 45.4 %all-gather.7.cloned.1.call-start = ((), (), s32[]{:S(2)}) async-start(), calls=%async_computation.8 | async-start | bytes 1572864 | tf_op jit(solution)/shard_map/all_gather | solution.py:28
  8.7 166.4 %reduce-scatter.11.cloned.1.call-start = ((), (), s32[]{:S(2)}) async-start(), calls=%async_computation.9 | async-start | bytes 3145728 | tf_op jit(solution)/shard_map/reduce_scatter | solution.py:32
  53.4 3.7 copy-start.19
  142.7 1.9 copy-start.9
  142.7 2.5 copy-start.31
  142.7 2.5 copy-start.32
  142.7 2.5 copy-start.33
  142.8 32.3 %copy-start.13 = (bf16[1024,256]{1,0:T(8,128)(2,1)S(1)}, bf16[1024,256]{1,0:T(8,128)(2,1)}, u32[]{:S(2)}) copy-start(bf16[1024,256]{1,0:T(8,128)(2,1)} %param.24) | copy-start | bytes 1572868
  144.6 38.9 %all-gather.11.cloned.1.call-start = ((), (), s32[]{:S(2)}) async-start(), calls=%async_computation.11 | async-start | bytes 1114112 | tf_op jit(solution)/shard_map/all_gather | solution.py:189
  145.2 60.4 %all-gather.9.cloned.1.call-start = ((), (), s32[]{:S(2)}) async-start(), calls=%async_computation.10 | async-start | bytes 1572864 | tf_op jit(solution)/shard_map/all_gather | solution.py:28
  145.3 38.2 %copy-start.28 = (bf16[1024]{0:T(1024)(128)(2,1)S(1)}, bf16[1024]{0:T(1024)(128)(2,1)}, u32[]{:S(2)}) copy-start(bf16[1024]{0:T(1024)(128)(2,1)} %param.33) | copy-start | bytes 6148
  182.9 62.7 %all-gather.13.cloned.1.call-start = ((), (), s32[]{:S(2)}) async-start(), calls=%async_computation.12 | async-start | bytes 1114112 | tf_op jit(solution)/shard_map/all_gather | solution.py:190
  183.4 97.6 %reduce-scatter.13.cloned.1.call-start = ((), (), s32[]{:S(2)}) async-start(), calls=%async_computation.13 | async-start | bytes 3145728 | tf_op jit(solution)/shard_map/reduce_scatter | solution.py:32
  250.0 37.9 %copy-start.8 = (bf16[1024,256]{1,0:T(8,128)(2,1)S(1)}, bf16[1024,256]{1,0:T(8,128)(2,1)}, u32[]{:S(2)}) copy-start(bf16[1024,256]{1,0:T(8,128)(2,1)} %param.38) | copy-start | bytes 1572868
  250.0 67.5 %all-gather.15.cloned.1.call-start = ((), (), s32[]{:S(2)}) async-start(), calls=%async_computation.14 | async-start | bytes 1572864 | tf_op jit(solution)/shard_map/all_gather | solution.py:28
  296.1 62.9 %reduce-scatter.15.cloned.1.call-start = ((), (), s32[]{:S(2)}) async-start(), calls=%async_computation.15 | async-start | bytes 3145728 | tf_op jit(solution)/shard_map/reduce_scatter | solution.py:32
  317.5 6.8 copy-start.30
  327.0 65.3 %all-gather.17.cloned.1.call-start = ((), (), s32[]{:S(2)}) async-start(), calls=%async_computation.16 | async-start | bytes 1572864 | tf_op jit(solution)/shard_map/all_gather | solution.py:28
  371.1 210.4 %reduce-scatter.17.cloned.1.call-start = ((), (), s32[]{:S(2)}) async-start(), calls=%async_computation.17 | async-start | bytes 3145728 | tf_op jit(solution)/shard_map/reduce_scatter | solution.py:32
  405.9 2.2 copy-start.3
  411.5 2.2 copy-start.3
  416.2 2.7 copy-start.5
  430.9 1.6 copy-start
  430.9 2.2 copy-start.3
  436.6 2.2 copy-start.3
  441.2 2.7 copy-start.5
  455.9 2.2 copy-start.3
  461.6 2.2 copy-start.3
  466.3 2.7 copy-start.5
  481.0 2.2 copy-start.3
  486.6 2.2 copy-start.3
  491.3 2.7 copy-start.5
  495.4 2.9 copy-start.20
  500.7 98.3 %reduce-scatter.23.cloned.1.call-start = ((), (), s32[]{:S(2)}) async-start(), calls=%async_computation.20 | async-start | bytes 2228224 | tf_op jit(solution)/shard_map/reduce_scatter | solution.py:301
  501.9 4.4 copy-start.18
  506.3 2.0 copy-start.15
  506.3 157.7 %reduce-scatter.21.cloned.1.call-start = ((), (), s32[]{:S(2)}) async-start(), calls=%async_computation.19 | async-start | bytes 2228224 | tf_op jit(solution)/shard_map/reduce_scatter | solution.py:300
  510.9 2.8 copy-start.17
  511.0 212.2 %reduce-scatter.19.cloned.1.call-start = ((), (), s32[]{:S(2)}) async-start(), calls=%async_computation.18 | async-start | bytes 557056 | tf_op jit(solution)/shard_map/reduce_scatter | solution.py:299
  513.7 272.4 %reduce-scatter.25.cloned.1.call-start = ((), (), s32[]{:S(2)}) async-start(), calls=%async_computation.21 | async-start | bytes 1671168
  517.1 3.3 copy-start.21
  517.1 3.3 copy-start.22
  517.1 3.3 copy-start.23
  517.1 3.3 copy-start.24
  517.1 3.3 copy-start.25
  517.2 3.3 copy-start.26
  517.2 3.3 copy-start.27
  517.2 64.3 %copy-start.11 = (f32[1024,256]{1,0:T(8,128)S(1)}, f32[1024,256]{1,0:T(8,128)}, u32[]{:S(2)}) copy-start(f32[1024,256]{1,0:T(8,128)} %get-tuple-element.478) | copy-start | bytes 3145732
  (55 other events, 66.7 us)
Sparse Core Ops, SparseCore 0:
  10.4 23.9 all-gather.6
  144.7 30.3 reduce-scatter.10
  296.2 21.2 all-gather.14
  327.1 31.8 reduce-scatter.14
Sparse Core Ops, SparseCore 1:
  147.3 36.2 all-gather.10
  185.5 20.1 all-gather.8
  207.7 37.8 all-gather.12
  250.1 30.8 reduce-scatter.12
  371.1 21.1 all-gather.16
  500.8 31.8 reduce-scatter.16
  536.9 62.1 reduce-scatter.22
  603.2 60.7 reduce-scatter.20
  667.9 55.1 reduce-scatter.18
  727.4 58.6 reduce-scatter.24
where the time goes:
time: 796 us; the launch traced here: 793 us
  waiting for transfers between devices  394 us (49%)
  local copies, waits for them, and re-layouts  152 us (19%)
  blocking collectives  125 us (16%)
  matrix products  76.9 us (10%)
  other arithmetic  27.7 us (3%)
  between operations  15.7 us (2%)
    reduce_scatter x4, waiting for transfers between devices, settle(): lax.psum_scatter(partial_value, 'col', scatter_dimension=1, tiled=True)  91.5 us
    reduce_scatter x1, waiting for transfers between devices, per_device(): lax.psum_scatter(ff1_grad_wide, 'row', scatter_dimension=0, tiled=True)  64.9 us
    unnamed x15, waiting for transfers between devices  64.8 us
    all_gather x4, waiting for transfers between devices, widen(): return lax.all_gather(shard, 'col', axis=1, tiled=True)  63.8 us
    psum x1, blocking collectives, per_device(): lax.psum((qkv_bias_grad, out_bias_grad, gain_one_grad, shift_one_grad, ff...  61 us
    reduce_scatter x1, waiting for transfers between devices, per_device(): lax.psum_scatter(out_grad_wide, 'row', scatter_dimension=1, tiled=True)  59.2 us
    dynamic_slice x24, local copies, waits for them, and re-layouts, attend_forward(): lax.map(one_group, (queries, keys_all, values_all, previous))  43.5 us
    while x120, local copies, waits for them, and re-layouts  41.6 us
  transfers between devices with their start and end apart: 14, of which 11 were waited for; matrix products, arithmetic and copies ran while one was open for 3% of the time, Pallas kernels for 0%

commit v1 on v0

v1 whole, which is shorter than its diff:
```python
import functools
import math

import jax
import jax.numpy as jnp
from jax import lax
from jax.experimental import pallas as pl
from jax.experimental.pallas import tpu as pltpu
from jax.sharding import PartitionSpec as P

DH = 64
F32 = jnp.float32
BF16 = jnp.bfloat16
norm_eps = 1e-06
root_half = 0.7071067811865476
inv_root_two_pi = 0.3989422804014327
NT = (((1,), (1,)), ((), ()))
TN = (((0,), (0,)), ((), ()))


def dot_nn(a, b):
    return jnp.dot(a, b, preferred_element_type=F32)


def dot_nt(a, b):
    return lax.dot_general(a, b, NT, preferred_element_type=F32)


def dot_tn(a, b):
    return lax.dot_general(a, b, TN, preferred_element_type=F32)


def pick(value, index, width):
    if width == DH:
        return value
    lane = lax.broadcasted_iota(jnp.int32, value.shape, 1)
    keep = (lane >= index * DH) & (lane < (index + 1) * DH)
    return jnp.where(keep, value, jnp.zeros_like(value))


def part_of(proj, pair, heads, part):
    pieces = [
        proj[:, (pair * heads + i) * 3 * DH + part * DH :][:, :DH] for i in range(heads)
    ]
    return pieces[0] if heads == 1 else jnp.concatenate(pieces, axis=1)


def forward_block(q_rows, k_all, v_masked, prev, width):
    raws, probs, total = [], [], None
    for i in range(width // DH):
        scores = dot_nt(pick(q_rows, i, width), k_all) + prev[i].astype(F32)
        raws.append(scores.astype(BF16))
        exponent = jnp.exp(scores - jnp.max(scores, axis=1, keepdims=True))
        scale = 1.0 / jnp.sum(exponent, axis=1, keepdims=True)
        prob = (exponent * scale).astype(BF16)
        probs.append(prob)
        out = dot_nn(prob, v_masked[i])
        total = out if total is None else total + out
    return raws, probs, total


def attend_forward_kernel(heads, pairs, proj_ref, prev_ref, raw_ref, prob_ref, out_ref, q_s, k_s, v_s):
    width = heads * DH
    rows = prev_ref.shape[1]
    block = pl.program_id(1)

    @pl.when(block == 0)
    def _():
        for pair in range(pairs):

            @pl.when(lax.rem(pl.program_id(0), pairs) == pair)
            def _():
                proj = proj_ref[...]
                q_s[...] = part_of(proj, pair, heads, 0) * jnp.asarray(0.125, BF16)
                k_s[...] = part_of(proj, pair, heads, 1)
                v = part_of(proj, pair, heads, 2)
                for i in range(heads):
                    v_s[i] = pick(v, i, width)

    q_rows = q_s[pl.ds(pl.multiple_of(block * rows, rows), rows), :]
    raws, probs, out = forward_block(
        q_rows, k_s[...], [v_s[i] for i in range(heads)], [prev_ref[i] for i in range(heads)], width
    )
    for i in range(heads):
        raw_ref[i] = raws[i]
        prob_ref[i] = probs[i]
    out_ref[...] = out.astype(BF16)


def attend_forward(proj, prev, seqs, head_count, rows):
    heads = min(2, head_count)
    pairs = head_count // heads
    length = prev.shape[-1]
    width = heads * DH
    group = lambda g, b: (g, b, 0)
    return pl.pallas_call(
        functools.partial(attend_forward_kernel, heads, pairs),
        grid=(seqs * pairs, length // rows),
        in_specs=[
            pl.BlockSpec((length, proj.shape[1]), lambda g, b: (g // pairs, 0)),
            pl.BlockSpec((heads, rows, length), group),
        ],
        out_specs=[
            pl.BlockSpec((heads, rows, length), group),
            pl.BlockSpec((heads, rows, length), group),
            pl.BlockSpec((rows, width), lambda g, b: ((g // pairs) * (length // rows) + b, g % pairs)),
        ],
        out_shape=[
            jax.ShapeDtypeStruct(prev.shape, BF16),
            jax.ShapeDtypeStruct(prev.shape, BF16),
            jax.ShapeDtypeStruct((seqs * length, head_count * DH), BF16),
        ],
        scratch_shapes=[
            pltpu.VMEM((length, width), BF16),
            pltpu.VMEM((length, width), BF16),
            pltpu.VMEM((heads, length, width), BF16),
        ],
        name="attend_forward",
    )(proj, prev)


def attend_backward_kernel(
    heads, pairs, proj_ref, prob_ref, grad_ref, cot_ref, pg_ref, dproj_ref, q_s, k_s, v_s, dq_s, dk_s, dv_s
):
    width = heads * DH
    rows = prob_ref.shape[1]
    block = pl.program_id(1)
    pair_now = lax.rem(pl.program_id(0), pairs)

    @pl.when(block == 0)
    def _():
        for pair in range(pairs):

            @pl.when(pair_now == pair)
            def _():
                proj = proj_ref[...]
                q_s[...] = part_of(proj, pair, heads, 0) * jnp.asarray(0.125, BF16)
                k = part_of(proj, pair, heads, 1)
                for i in range(heads):
                    k_s[i] = pick(k, i, width)
                v_s[...] = part_of(proj, pair, heads, 2)

        dk_s[...] = jnp.zeros_like(dk_s)
        dv_s[...] = jnp.zeros_like(dv_s)

    at = pl.ds(pl.multiple_of(block * rows, rows), rows)
    q_rows = q_s[at, :]
    d_rows = grad_ref[...]
    dq = None
    dk = None
    dv = None
    for i in range(heads):
        d_one = pick(d_rows, i, width)
        d_probs = dot_nt(d_one, v_s[...])
        prob = prob_ref[i]
        wide = prob.astype(F32)
        delta = jnp.sum(d_probs * wide, axis=1, keepdims=True)
        low = (wide * (d_probs - delta) + cot_ref[i].astype(F32)).astype(BF16)
        pg_ref[i] = low
        a = dot_nn(low, k_s[i])
        b = dot_tn(pick(q_rows, i, width), low)
        c = dot_tn(d_one, prob)
        dq = a if dq is None else dq + a
        dk = b if dk is None else dk + b
        dv = c if dv is None else dv + c
    dq_s[at, :] = (dq * 0.125).astype(BF16)
    dk_s[...] += dk
    dv_s[...] += dv

    @pl.when(block == pl.num_programs(1) - 1)
    def _():
        for pair in range(pairs):

            @pl.when(pair_now == pair)
            def _():
                parts = [dq_s[...], dk_s[...].T.astype(BF16), dv_s[...].T.astype(BF16)]
                for i in range(heads):
                    base = (pair * heads + i) * 3 * DH
                    dproj_ref[:, base : base + 3 * DH] = jnp.concatenate(
                        [p[:, i * DH : (i + 1) * DH] for p in parts], axis=1
                    )


def attend_backward(proj, prob, grad, cot, seqs, head_count, rows):
    heads = min(2, head_count)
    pairs = head_count // heads
    length = prob.shape[-1]
    width = heads * DH
    group = lambda g, b: (g, b, 0)
    return pl.pallas_call(
        functools.partial(attend_backward_kernel, heads, pairs),
        grid=(seqs * pairs, length // rows),
        in_specs=[
            pl.BlockSpec((length, proj.shape[1]), lambda g, b: (g // pairs, 0)),
            pl.BlockSpec((heads, rows, length), group),
            pl.BlockSpec((rows, width), lambda g, b: ((g // pairs) * (length // rows) + b, g % pairs)),
            pl.BlockSpec((heads, rows, length), group),
        ],
        out_specs=[
            pl.BlockSpec((heads, rows, length), group),
            pl.BlockSpec((length, proj.shape[1]), lambda g, b: (g // pairs, 0)),
        ],
        out_shape=[
            jax.ShapeDtypeStruct(prob.shape, BF16),
            jax.ShapeDtypeStruct(proj.shape, BF16),
        ],
        scratch_shapes=[
            pltpu.VMEM((length, width), BF16),
            pltpu.VMEM((heads, length, width), BF16),
            pltpu.VMEM((length, width), BF16),
            pltpu.VMEM((length, width), BF16),
            pltpu.VMEM((width, length), F32),
            pltpu.VMEM((width, length), F32),
        ],
        name="attend_backward",
    )(proj, prob, grad, cot)


def normalize(hidden):
    width = hidden.shape[1]
    center = hidden - jnp.sum(hidden, axis=1, keepdims=True) * (1.0 / width)
    inv_std = lax.rsqrt(jnp.sum(center * center, axis=1, keepdims=True) * (1.0 / width) + norm_eps)
    return center * inv_std, inv_std


def norm_back(scaled, xhat, inv_std):
    width = scaled.shape[1]
    mean_grad = jnp.sum(scaled, axis=1, keepdims=True) * (1.0 / width)
    mean_cross = jnp.sum(scaled * xhat, axis=1, keepdims=True) * (1.0 / width)
    return inv_std * (scaled - mean_grad - xhat * mean_cross)


def col_sum(value):
    return jnp.sum(value, axis=0, keepdims=True)


def middle_kernel(
    tok_ref, att_ref, og_ref, w_ref, vec_ref, ffb_ref, out_ref, dh_ref, datt_ref, gw_ref, gvec_ref, gffb_ref, act_s, slope_s
):
    cols = w_ref.shape[0]
    width = vec_ref.shape[1]
    hw = width // cols
    fw = ffb_ref.shape[1] // cols
    cut = min(512, fw)
    att = [att_ref[:, c * hw : (c + 1) * hw] for c in range(cols)]
    vec = vec_ref[...].astype(F32)
    out_bias, gain1, shift1, ff2_bias, gain2, shift2 = (vec[i : i + 1] for i in range(6))

    branch = None
    for c in range(cols):
        t = dot_nt(att[c], w_ref[c, :, :hw])
        branch = t if branch is None else branch + t
    hidden1 = tok_ref[...].astype(F32) + branch + out_bias
    xhat1, inv1 = normalize(hidden1)
    normed1 = xhat1 * gain1 + shift1
    low1 = normed1.astype(BF16)

    chunks = [(c, o) for c in range(cols) for o in range(0, fw, cut)]
    hidden2 = normed1 + ff2_bias
    for c, o in chunks:
        at = c * fw + o
        inner = dot_nn(low1, w_ref[c, :, hw + o : hw + o + cut]) + ffb_ref[:, at : at + cut].astype(F32)
        half = 0.5 + 0.5 * lax.erf(inner * root_half)
        act = (inner * half).astype(BF16)
        act_s[:, at : at + cut] = act
        slope_s[:, at : at + cut] = half + inner * inv_root_two_pi * jnp.exp(-0.5 * inner * inner)
        hidden2 = hidden2 + dot_nt(act, w_ref[c, :, hw + fw + o : hw + fw + o + cut])
    xhat2, inv2 = normalize(hidden2)
    out_ref[...] = (xhat2 * gain2 + shift2).astype(BF16)

    og = og_ref[...].astype(F32)
    d_hidden2 = norm_back(og * gain2, xhat2, inv2)
    low2 = d_hidden2.astype(BF16)
    rows = [None] * 6
    rows[4] = col_sum(og * xhat2)
    rows[5] = col_sum(og)
    rows[3] = col_sum(low2.astype(F32))
    low1_t = low1.T
    low2_t = low2.T
    d_normed1 = d_hidden2
    for c, o in chunks:
        at = c * fw + o
        d_act = dot_nn(low2, w_ref[c, :, hw + fw + o : hw + fw + o + cut])
        d_inner = (d_act * slope_s[:, at : at + cut]).astype(BF16)
        d_normed1 = d_normed1 + dot_nt(d_inner, w_ref[c, :, hw + o : hw + o + cut])
        gw_ref[c, :, hw + o : hw + o + cut] = dot_nn(low1_t, d_inner).astype(BF16)
        gw_ref[c, :, hw + fw + o : hw + fw + o + cut] = dot_nn(low2_t, act_s[:, at : at + cut]).astype(BF16)
        gffb_ref[:, at : at + cut] = col_sum(d_inner.astype(F32))

    rows[1] = col_sum(d_normed1 * xhat1)
    rows[2] = col_sum(d_normed1)
    d_hidden1 = norm_back(d_normed1 * gain1, xhat1, inv1)
    dh_ref[...] = d_hidden1.astype(dh_ref.dtype)
    low = d_hidden1.astype(BF16)
    rows[0] = col_sum(low.astype(F32))
    low_t = low.T
    for c in range(cols):
        datt_ref[:, c * hw : (c + 1) * hw] = dot_nn(low, w_ref[c, :, :hw]).astype(BF16)
        gw_ref[c, :, :hw] = dot_nn(low_t, att[c]).astype(BF16)
    gvec_ref[...] = jnp.concatenate(rows, axis=0)


def middle(tok, att, og, w, vec, ffb):
    rows, width = tok.shape
    hidden = ffb.shape[1]
    return pl.pallas_call(
        middle_kernel,
        out_shape=[
            jax.ShapeDtypeStruct((rows, width), BF16),
            jax.ShapeDtypeStruct((rows, width), F32),
            jax.ShapeDtypeStruct((rows, width), BF16),
            jax.ShapeDtypeStruct(w.shape, BF16),
            jax.ShapeDtypeStruct((6, width), F32),
            jax.ShapeDtypeStruct((1, hidden), F32),
        ],
        in_specs=[pl.BlockSpec(memory_space=pltpu.VMEM)] * 6,
        out_specs=[pl.BlockSpec(memory_space=pltpu.VMEM)] * 6,
        scratch_shapes=[pltpu.VMEM((rows, hidden), BF16), pltpu.VMEM((rows, hidden), F32)],
        compiler_params=pltpu.CompilerParams(vmem_limit_bytes=60 << 20),
        name="middle",
    )(tok, att, og, w, vec, ffb)


def per_device(
    cols,
    tokens,
    prev_logits,
    qkv_weight,
    qkv_bias,
    out_weight,
    out_bias,
    norm1_gain,
    norm1_shift,
    ff1_weight,
    ff1_bias,
    ff2_weight,
    ff2_bias,
    norm2_gain,
    norm2_shift,
    out_grad,
    logit_grad,
):
    seqs, head_count, length, _ = prev_logits.shape
    total, feat = tokens.shape
    share = total // cols
    rows = min(256, length)
    me = lax.axis_index("col")

    def to_rows(x):
        return lax.all_to_all(x, "col", split_axis=0, concat_axis=1, tiled=True)

    def to_features(x):
        return lax.all_to_all(x, "col", split_axis=1, concat_axis=0, tiled=True)

    tokens_full = lax.all_gather(tokens, "col", axis=1, tiled=True)
    wide_qkv = lax.all_gather(qkv_weight, "row", axis=0, tiled=True)
    mixed = jnp.concatenate([out_weight.T, ff1_weight, ff2_weight.T], axis=1)
    mixed = lax.all_gather(lax.all_gather(mixed, "row", axis=0, tiled=True), "col", axis=0)
    vectors = jnp.stack([out_bias, norm1_gain, norm1_shift, ff2_bias, norm2_gain, norm2_shift])
    vectors = lax.all_gather(vectors, "col", axis=1, tiled=True)
    ff1_bias_full = lax.all_gather(ff1_bias, "col", axis=0, tiled=True)[None]
    og = to_rows(out_grad)

    proj = (dot_nn(tokens_full, wide_qkv) + qkv_bias.astype(F32)).astype(BF16)
    prev = prev_logits.reshape(seqs * head_count, length, length)
    cot = logit_grad.reshape(seqs * head_count, length, length)
    raw, prob, att = attend_forward(proj, prev, seqs, head_count, rows)
    att_rows = to_rows(att)
    tok_rows = lax.dynamic_slice_in_dim(tokens_full, me * share, share, 0)
    out, dh, datt, gw, gvec, gffb = middle(tok_rows, att_rows, og, mixed, vectors, ff1_bias_full)
    output = to_features(out)
    d_hidden = to_features(dh)
    datt_full = to_features(datt)
    prev_grad, dproj = attend_backward(proj, prob, datt_full, cot, seqs, head_count, rows)

    input_part = lax.psum_scatter(
        dot_nt(dproj, wide_qkv), "col", scatter_dimension=1, tiled=True
    )
    input_grad = (d_hidden + input_part).astype(BF16)
    qkv_grad = lax.psum_scatter(dot_tn(tokens_full, dproj), "row", scatter_dimension=0, tiled=True)
    qkv_bias_grad = jnp.sum(dproj.astype(F32), axis=0)
    gw = lax.psum_scatter(gw.astype(F32), "row", scatter_dimension=1, tiled=True)
    gw = lax.psum_scatter(gw, "col", scatter_dimension=0, tiled=True)[0]
    hidden = ff1_weight.shape[1]
    vec_sum = lax.psum_scatter(
        jnp.concatenate(
            [gvec.reshape(6, cols, feat).transpose(1, 0, 2).reshape(cols, 6 * feat), gffb.reshape(cols, hidden)],
            axis=1,
        ),
        "col",
        scatter_dimension=0,
        tiled=True,
    )[0]
    vec_sum, qkv_bias_grad = lax.psum((vec_sum, qkv_bias_grad), "row")
    vs = [vec_sum[i * feat : (i + 1) * feat] for i in range(6)]
    return (
        output,
        raw.reshape(prev_logits.shape),
        input_grad,
        prev_grad.reshape(prev_logits.shape),
        qkv_grad,
        qkv_bias_grad,
        gw[:, :feat].T,
        vs[0],
        vs[1],
        vs[2],
        gw[:, feat : feat + hidden],
        vec_sum[6 * feat :],
        gw[:, feat + hidden :].T,
        vs[3],
        vs[4],
        vs[5],
    )


def solution(mesh):
    in_specs = (
        P("row", "col"),
        P("row", "col", None, None),
        P("row", "col"),
        P("col"),
        P("col", "row"),
        P("col"),
        P("col"),
        P("col"),
        P("row", "col"),
        P("col"),
        P("col", "row"),
        P("col"),
        P("col"),
        P("col"),
        P("row", "col"),
        P("row", "col", None, None),
    )
    out_specs = (
        P("row", "col"),
        P("row", "col", None, None),
        P("row", "col"),
        P("row", "col", None, None),
        P("row", "col"),
        P("col"),
        P("col", "row"),
        P("col"),
        P("col"),
        P("col"),
        P("row", "col"),
        P("col"),
        P("col", "row"),
        P("col"),
        P("col"),
        P("col"),
    )
    return jax.shard_map(
        functools.partial(per_device, mesh.shape["col"]),
        mesh=mesh,
        in_specs=in_specs,
        out_specs=out_specs,
        check_vma=False,
    )
```

time: 796 us -> 419 us (0.53)
  waiting for transfers between devices: 394 us -> 166 us
  local copies, waits for them, and re-layouts: 152 us -> 15.7 us
  matrix products: 76.9 us -> 9.3 us
  Pallas kernels: 0 us -> 49.6 us
  other arithmetic: 27.7 us -> 11.4 us
  starting transfers between devices: 0.77 us -> 14.5 us
  blocking collectives: 125 us -> 137 us
    reduce_scatter x7 -> x3, waiting for transfers between devices: 231 us -> 76.8 us  [the longest x1 76.8 us: per_device(): lax.psum_scatter(gw.astype(F32), 'row', scatter_dimension=1, tiled=True)]
    dot_general x68 -> x3, matrix products: 76.9 us -> 9.3 us  [the longest x1 3.72 us: dot_nt(): return lax.dot_general(a, b, NT, preferred_element_type=F32)]
    unnamed x15 -> x8, waiting for transfers between devices: 64.8 us -> 11.7 us
    pallas_call x0 -> x3, Pallas kernels: none -> 49.6 us  [the longest x1 18.4 us: attend_backward(): pl.pallas_call(functools.partial(attend_backward_kernel, heads, pairs), g...]
    dynamic_slice x36 -> x1, local copies, waits for them, and re-layouts: 46.5 us -> 0.83 us  [per_device(): tok_rows = lax.dynamic_slice_in_dim(tokens_full, me * share, share, 0)]
    while x124 -> x0, local copies, waits for them, and re-layouts: 42.2 us -> none
    all_gather x6 -> x3, waiting for transfers between devices: 98 us -> 66.2 us  [the longest x1 46.3 us: per_device(): lax.all_gather(mixed, 'row', axis=0, tiled=True)]
    dynamic_update_slice x36 -> x0, local copies, waits for them, and re-layouts: 31.2 us -> none  [the longest x16 15.8 us: attend_backward(): lax.map(one_group, (queries, keys_all, values_all, previous, log_totals,...]
  transfers between devices with their start and end apart: 14 -> 11, of which waited for: 11 -> 5; matrix products, arithmetic and copies ran while one was open for 3% -> 6% of each run, Pallas kernels for 0% -> 8%
where the time goes in v1:
time: 419 us; the launch traced here: 418 us
  waiting for transfers between devices  166 us (40%)
  blocking collectives  137 us (33%)
  Pallas kernels  49.6 us (12%)
  local copies, waits for them, and re-layouts  15.7 us (4%)
  starting transfers between devices  14.5 us (3%)
  between operations  14.4 us (3%)
  other arithmetic  11.4 us (3%)
  matrix products  9.3 us (2%)
    reduce_scatter x1, waiting for transfers between devices, per_device(): lax.psum_scatter(gw.astype(F32), 'row', scatter_dimension=1, tiled=True)  76.8 us
    psum x1, blocking collectives, per_device(): vec_sum, qkv_bias_grad = lax.psum((vec_sum, qkv_bias_grad), 'row')  60.6 us
    all_gather x1, waiting for transfers between devices, per_device(): lax.all_gather(mixed, 'row', axis=0, tiled=True)  46.3 us
    unnamed x1, blocking collectives  23.6 us
    all_gather x1, blocking collectives, per_device(): wide_qkv = lax.all_gather(qkv_weight, 'row', axis=0, tiled=True)  21.3 us
    all_gather x1, waiting for transfers between devices, per_device(): lax.all_gather(lax.all_gather(mixed, 'row', axis=0, tiled=True), 'col', a...  19.9 us
    pallas_call x1, Pallas kernels, attend_backward(): pl.pallas_call(functools.partial(attend_backward_kernel, heads, pairs), g...  18.4 us
    pallas_call x1, Pallas kernels, attend_forward(): pl.pallas_call(functools.partial(attend_forward_kernel, heads, pairs), gr...  16.6 us
  transfers between devices with their start and end apart: 11, of which 5 were waited for; matrix products, arithmetic and copies ran while one was open for 6% of the time, Pallas kernels for 8%

profile of v1, /device:TPU:0, one launch (start us, length us, event | category | flops | bytes accessed | tf_op | source)
XLA Modules:
  0.0 417.9 jit_solution(10819972254629947105)
XLA Ops:
  7.2 0.0 all-gather.7.cloned.1.call-start
  7.2 1.5 pad_maximum_fusion
  8.8 0.0 all-gather.5.cloned.1.call-start
  8.8 0.7 all-gather.5.cloned.1.call-update
  9.6 46.3 %all-gather.7.cloned.1.call-done = bf16[512,2304]{1,0:T(8,128)(2,1)} async-done(((bf16[32,2304]{1,0:T(8,128)(2,1)}), bf16[512,2304]{1,0:T(8,128)(2,1)}) %all-gather.7.cloned.1.call-update) | async-done | bytes 2359312 | tf_op jit(solution)/shard_map/all_gather | solution.py:358
  55.9 3.5 all-to-all-start.1
  59.5 21.3 %all_gather.22 = bf16[512,768]{1,0:T(8,128)(2,1)S(1)} all-gather(bf16[32,768]{1,0:T(8,128)(2,1)S(1)} %copy-done.4), channel_id=1, replica_groups=mesh['row'=16,'col'=2] {'row'}, dimensions={0}, use_global_device_ids=true | all-gather | bytes 835584 | tf_op jit(solution)/shard_map/all_gather | solution.py:356
  80.8 3.3 add_convert_fusion.proj_ref
  84.2 16.6 %attend_forward.1 = (bf16[4,1024,1024]{2,1,0:T(8,128)(2,1)}, bf16[4,1024,1024]{2,1,0:T(8,128)(2,1)}, bf16[1024,256]{1,0:T(8,128)(2,1)}) custom-call(bf16[1024,768]{1,0:T(8,128)(2,1)} %add_convert_fusion.proj_ref, bf16[4,1024,1024]{2,1,0:T(8,128)(2,1)} %bitcast.57), custom_call_target="tpu_custom_call" | custom-call | tf_op jit(solution)/shard_map/attend_forward/pallas_call | solution.py:96
  100.7 3.6 all-to-all-start
  104.4 0.0 reduce-scatter.9.cloned.1.call-start
  104.6 14.9 %all_gather.27 = bf16[2048]{0:T(1024)(128)(2,1)S(1)} all-gather(bf16[1024]{0:T(1024)(128)(2,1)S(1)} %copy-done.8), channel_id=1, replica_groups=mesh['row'=16,'col'=2] {'col'}, dimensions={0}, use_global_device_ids=true | all-gather | bytes 6144 | tf_op jit(solution)/shard_map/all_gather | solution.py:361
  119.5 0.6 broadcast_in_dim.4.ffb_ref
  120.1 4.9 %all_gather.26.vec_ref = bf16[6,512]{1,0:T(8,128)(2,1)} all-gather(bf16[6,256]{1,0:T(8,128)(2,1)S(1)} %stack.27), channel_id=1, replica_groups=mesh['row'=16,'col'=2] {'col'}, dimensions={1}, use_global_device_ids=true | all-gather | bytes 9216 | tf_op jit(solution)/shard_map/all_gather | solution.py:360
  125.0 0.8 copy.50
  125.8 0.8 constant_dynamic-slice_fusion.tok_ref
  126.7 0.8 copy.49
  127.5 19.9 %all-gather.9.cloned.1.call-done = bf16[1024,2304]{1,0:T(8,128)(2,1)} async-done(((bf16[512,2304]{1,0:T(8,128)(2,1)}), bf16[1024,2304]{1,0:T(8,128)(2,1)}) %all-gather.9.cloned.1.call-update) | async-done | bytes 4718608 | tf_op jit(solution)/shard_map/all_gather | solution.py:358
  147.4 14.6 %middle.1 = (bf16[512,512]{1,0:T(8,128)(2,1)}, f32[512,512]{1,0:T(8,128)}, bf16[512,512]{1,0:T(8,128)(2,1)}, bf16[2,512,2304]{2,1,0:T(8,128)(2,1)}, f32[6,512]{1,0:T(8,128)}, /*index=5*/f32[1,2048]{1,0:T(1,128)}) custom-call(bf16[512,512]{1,0:T(8,128)(2,1)} %constant_dynamic-slice_fusion.tok_ref, bf16[512,512]{1,0:T(8,128)(2,1)} %bitcast.61, ...), custom_call_target="tpu_custom_call" | custom-call | tf_op jit(solution)/shard_map/middle/pallas_call | solution.py:306
  162.0 6.7 %convert_element_type.19 = f32[2,512,2304]{2,1,0:T(8,128)} convert(bf16[2,512,2304]{2,1,0:T(8,128)(2,1)} %get-tuple-element.35) | non-fusion elementwise | flops 2359296 | bytes 14155776 | tf_op jit(solution)/shard_map/convert_element_type | solution.py:382
  168.8 0.0 reduce-scatter.7.cloned.1.call-start
  168.8 1.0 copy-done.2
  169.8 11.2 %all_to_all.95 = bf16[512,2,256]{2,0,1:T(8,128)(2,1)} all-to-all(bf16[512,2,256]{2,0,1:T(8,128)(2,1)S(1)} %bitcast.66), channel_id=1, replica_groups=mesh['row'=16,'col'=2] {'col'}, dimensions={1} | all-to-all | bytes 1048576 | tf_op jit(solution)/shard_map/all_to_all | solution.py:353
  181.1 18.4 %attend_backward.1 = (bf16[4,1024,1024]{2,1,0:T(8,128)(2,1)}, bf16[1024,768]{1,0:T(8,128)(2,1)}) custom-call(bf16[1024,768]{1,0:T(8,128)(2,1)} %add_convert_fusion.proj_ref, bf16[4,1024,1024]{2,1,0:T(8,128)(2,1)} %get-tuple-element.31.prob_ref, bf16[1024,256]{1,0:T(8,128)(2,1)} %bitcast.62, bf16[4,1024,1024]{2,1,0:T(8,128)(2,1)} %bitcast.58), custom_call_target="tpu_custom_call" | custom-call | tf_op jit(solution)/shard_map/attend_backward/pallas_call | solution.py:190
  199.5 3.7 fusion.2
  203.2 0.0 reduce-scatter.11.cloned.1.call-start
  203.3 76.8 %reduce-scatter.9.cloned.1.call-done = f32[2,32,2304]{2,1,0:T(8,128)} async-done(((f32[2,512,2304]{2,1,0:T(8,128)}), f32[2,32,2304]{2,1,0:T(8,128)}) %reduce-scatter.9.cloned.1.call-update) | async-done | bytes 589840 | tf_op jit(solution)/shard_map/reduce_scatter | solution.py:382
  280.1 2.2 convolution_bitcast_fusion
  282.4 1.6 copy.44
  284.1 2.0 copy.56
  286.0 3.5 all-to-all-start.2
  289.6 0.6 dynamic-slice
  290.2 1.1 copy.54
  291.2 0.5 broadcast.5
  291.7 0.7 reduce.5
  292.5 11.7 %all-to-all-done.2 = bf16[512,2,256]{2,0,1:T(8,128)(2,1)S(1)} async-done(((bf16[512,2,256]{2,0,1:T(8,128)(2,1)}), bf16[512,2,256]{2,0,1:T(8,128)(2,1)S(1)}, u32[]{:S(2)}, u32[]{:S(2)}) %all-to-all-start.2) | async-done | bytes 524320 | tf_op jit(solution)/shard_map/all_to_all | solution.py:353
  304.1 3.6 all-to-all-start.3
  307.7 23.6 %all-reduce = f32[2,2560]{1,0:T(2,128)S(1)} all-reduce(f32[2,2560]{1,0:T(2,128)S(1)} %pad_maximum_fusion.1), channel_id=7, replica_groups=mesh['row'=16,'col'=2] {'col'}, use_global_device_ids=true, to_apply=%region_6.0.clone | all-reduce | flops 5120 | bytes 40960
  331.4 0.7 dynamic-slice_reduce_fusion
  332.1 0.3 convert_reduce_fusion
  332.3 60.6 %all-reduce.1 = (f32[768]{0:T(1024)}, f32[2560]{0:T(1024)S(1)}) all-reduce(f32[768]{0:T(1024)S(1)} %convert_reduce_fusion, f32[2560]{0:T(1024)S(1)} %dynamic-slice_reduce_fusion), channel_id=1, replica_groups=mesh['row'=16,'col'=2] {'row'}, use_global_device_ids=true, to_apply=%region_3.0 | all-reduce | flops 3328 | bytes 26624 | tf_op jit(solution)/shard_map/psum | solution.py:394
  392.9 0.6 slice.45
  393.5 0.6 fusion.1
  394.1 2.2 fusion
  396.3 1.4 slice_bitcast_fusion.1
  397.7 1.7 slice_bitcast_fusion
  399.3 10.9 %reduce-scatter.13.cloned.1.call-done = f32[32,768]{1,0:T(8,128)} async-done(((f32[512,768]{1,0:T(8,128)}), f32[32,768]{1,0:T(8,128)}) %reduce-scatter.13.cloned.1.call-update) | async-done | bytes 98320
  410.3 0.8 copy.58
  (57 shorter events, 0.4 us)
Async XLA Ops:
  7.2 48.7 %all-gather.7.cloned.1.call-start = ((), (), s32[]{:S(2)}) async-start(), calls=%async_computation.10 | async-start | bytes 2506752 | tf_op jit(solution)/shard_map/all_gather | solution.py:358
  8.8 50.7 %copy-start.7 = (bf16[768]{0:T(1024)(128)(2,1)S(1)}, bf16[768]{0:T(1024)(128)(2,1)}, u32[]{:S(2)}) copy-start(bf16[768]{0:T(1024)(128)(2,1)} %param.19) | copy-start | bytes 4612
  8.8 50.7 %copy-start.4 = (bf16[32,768]{1,0:T(8,128)(2,1)S(1)}, bf16[32,768]{1,0:T(8,128)(2,1)}, u32[]{:S(2)}) copy-start(bf16[32,768]{1,0:T(8,128)(2,1)} %param.18) | copy-start | bytes 147460
  8.8 72.0 %all-gather.5.cloned.1.call-start = ((), (), s32[]{:S(2)}) async-start(), calls=%async_computation.9 | async-start | bytes 1572864 | tf_op jit(solution)/shard_map/all_gather | solution.py:355
  9.6 137.9 %all-gather.9.cloned.1.call-start = ((), (), s32[]{:S(2)}) async-start(), calls=%async_computation.14 | async-start | bytes 7077888 | tf_op jit(solution)/shard_map/all_gather | solution.py:358
  55.9 44.8 %all-to-all-start.1 = ((bf16[2,512,256]{2,1,0:T(8,128)(2,1)}), bf16[2,512,256]{2,1,0:T(8,128)(2,1)S(1)}, u32[]{:S(2)}, u32[]{:S(2)}) async-start(bf16[2,512,256]{2,1,0:T(8,128)(2,1)} %bitcast.3), calls=%async_computation.1 | async-start | bytes 1048576 | tf_op jit(solution)/shard_map/all_to_all | solution.py:350
  84.1 20.3 %copy-start.9 = (bf16[256]{0:T(256)(128)(2,1)S(1)}, bf16[256]{0:T(256)(128)(2,1)}, u32[]{:S(2)}) copy-start(bf16[256]{0:T(256)(128)(2,1)} %param.21) | copy-start | bytes 1540
  84.1 20.4 %copy-start.10 = (bf16[256]{0:T(256)(128)(2,1)S(1)}, bf16[256]{0:T(256)(128)(2,1)}, u32[]{:S(2)}) copy-start(bf16[256]{0:T(256)(128)(2,1)} %param.22) | copy-start | bytes 1540
  84.1 20.4 %copy-start.11 = (bf16[256]{0:T(256)(128)(2,1)S(1)}, bf16[256]{0:T(256)(128)(2,1)}, u32[]{:S(2)}) copy-start(bf16[256]{0:T(256)(128)(2,1)} %param.23) | copy-start | bytes 1540
  84.1 20.4 %copy-start.12 = (bf16[256]{0:T(256)(128)(2,1)S(1)}, bf16[256]{0:T(256)(128)(2,1)}, u32[]{:S(2)}) copy-start(bf16[256]{0:T(256)(128)(2,1)} %param.27) | copy-start | bytes 1540
  84.1 20.4 %copy-start.13 = (bf16[256]{0:T(256)(128)(2,1)S(1)}, bf16[256]{0:T(256)(128)(2,1)}, u32[]{:S(2)}) copy-start(bf16[256]{0:T(256)(128)(2,1)} %param.28) | copy-start | bytes 1540
  84.1 20.4 %copy-start.14 = (bf16[256]{0:T(256)(128)(2,1)S(1)}, bf16[256]{0:T(256)(128)(2,1)}, u32[]{:S(2)}) copy-start(bf16[256]{0:T(256)(128)(2,1)} %param.29) | copy-start | bytes 1540
  84.1 20.4 %copy-start.8 = (bf16[1024]{0:T(1024)(128)(2,1)S(1)}, bf16[1024]{0:T(1024)(128)(2,1)}, u32[]{:S(2)}) copy-start(bf16[1024]{0:T(1024)(128)(2,1)} %param.25) | copy-start | bytes 6148
  100.7 25.1 %copy-start.3 = (bf16[1024,512]{1,0:T(8,128)(2,1)S(1)}, bf16[1024,512]{1,0:T(8,128)(2,1)}, u32[]{:S(2)}) copy-start(bf16[1024,512]{1,0:T(8,128)(2,1)} %all-gather.5.cloned.1.call-done) | copy-start | bytes 3145732
  100.7 25.9 %all-to-all-start = ((bf16[2,512,256]{2,1,0:T(8,128)(2,1)}), bf16[2,512,256]{2,1,0:T(8,128)(2,1)S(1)}, u32[]{:S(2)}, u32[]{:S(2)}) async-start(bf16[2,512,256]{2,1,0:T(8,128)(2,1)} %bitcast.69), calls=%async_computation | async-start | bytes 1048576 | tf_op jit(solution)/shard_map/all_to_all | solution.py:350
  104.4 175.7 %reduce-scatter.9.cloned.1.call-start = ((), (), s32[]{:S(2)}) async-start(), calls=%async_computation.12 | async-start | bytes 10027008 | tf_op jit(solution)/shard_map/reduce_scatter | solution.py:382
  168.8 1.0 copy-start.2
  168.8 225.3 %reduce-scatter.7.cloned.1.call-start = ((), (), s32[]{:S(2)}) async-start(), calls=%async_computation.11 | async-start | bytes 3145728 | tf_op jit(solution)/shard_map/reduce_scatter | solution.py:376
  203.2 77.0 %copy-start = (bf16[1024,768]{1,0:T(8,128)(2,1)S(1)}, bf16[1024,768]{1,0:T(8,128)(2,1)}, u32[]{:S(2)}) copy-start(bf16[1024,768]{1,0:T(8,128)(2,1)} %get-tuple-element.33) | copy-start | bytes 4718596
  203.2 193.1 %reduce-scatter.11.cloned.1.call-start = ((), (), s32[]{:S(2)}) async-start(), calls=%async_computation.13 | async-start | bytes 884736 | tf_op jit(solution)/shard_map/reduce_scatter | solution.py:383
  280.1 130.2 %reduce-scatter.13.cloned.1.call-start = ((), (), s32[]{:S(2)}) async-start(), calls=%async_computation.15 | async-start | bytes 1671168
  284.0 5.6 %copy-start.15 = (u32[32]{0:T(128)S(1)}, u32[32]{0:T(128)}, u32[]{:S(2)}) copy-start(u32[32]{0:T(128)} %constant.16) | copy-start | bytes 388
  284.0 6.1 %copy-start.1 = (f32[512,512]{1,0:T(8,128)S(1)}, f32[512,512]{1,0:T(8,128)}, u32[]{:S(2)}) copy-start(f32[512,512]{1,0:T(8,128)} %get-tuple-element.30) | copy-start | bytes 3145732
  284.0 7.7 %copy-start.6 = (f32[1,2048]{1,0:T(1,128)S(1)}, f32[1,2048]{1,0:T(1,128)}, u32[]{:S(2)}) copy-start(f32[1,2048]{1,0:T(1,128)} %get-tuple-element.37) | copy-start | bytes 24580
  284.0 8.4 %copy-start.5 = (f32[6,512]{1,0:T(8,128)S(1)}, f32[6,512]{1,0:T(8,128)}, u32[]{:S(2)}) copy-start(f32[6,512]{1,0:T(8,128)} %get-tuple-element.36) | copy-start | bytes 36868
  286.0 18.1 %all-to-all-start.2 = ((bf16[512,2,256]{2,0,1:T(8,128)(2,1)}), bf16[512,2,256]{2,0,1:T(8,128)(2,1)S(1)}, u32[]{:S(2)}, u32[]{:S(2)}) async-start(bf16[512,2,256]{2,0,1:T(8,128)(2,1)} %bitcast.56), calls=%async_computation.2 | async-start | bytes 1048576 | tf_op jit(solution)/shard_map/all_to_all | solution.py:353
  304.1 90.0 %all-to-all-start.3 = ((f32[512,2,256]{2,0,1:T(8,128)}), f32[512,2,256]{2,0,1:T(8,128)S(1)}, u32[]{:S(2)}, u32[]{:S(2)}) async-start(f32[512,2,256]{2,0,1:T(8,128)} %bitcast.54), calls=%async_computation.3 | async-start | bytes 2097152 | tf_op jit(solution)/shard_map/all_to_all | solution.py:353
Sparse Core Ops, SparseCore 0:
  10.8 45.0 all-gather.6
  57.4 22.0 all-gather.4
  81.1 66.2 all-gather.8
  168.9 111.1 reduce-scatter.8
  282.2 45.1 reduce-scatter.6
  329.4 16.7 reduce-scatter.10
  350.5 59.7 reduce-scatter.12

commit v2 on v1

v2 whole, which is shorter than its diff:
```python
import functools
import math

import jax
import jax.numpy as jnp
from jax import lax
from jax.experimental import pallas as pl
from jax.experimental.pallas import tpu as pltpu
from jax.sharding import PartitionSpec as P

DH = 64
F32 = jnp.float32
BF16 = jnp.bfloat16
norm_eps = 1e-06
root_half = 0.7071067811865476
inv_root_two_pi = 0.3989422804014327
NT = (((1,), (1,)), ((), ()))
TN = (((0,), (0,)), ((), ()))


def dot_nn(a, b):
    return jnp.dot(a, b, preferred_element_type=F32)


def dot_nt(a, b):
    return lax.dot_general(a, b, NT, preferred_element_type=F32)


def dot_tn(a, b):
    return lax.dot_general(a, b, TN, preferred_element_type=F32)


def pick(value, index, width):
    if width == DH:
        return value
    lane = lax.broadcasted_iota(jnp.int32, value.shape, 1)
    keep = (lane >= index * DH) & (lane < (index + 1) * DH)
    return jnp.where(keep, value, jnp.zeros_like(value))


def part_of(proj, pair, heads, part):
    pieces = [
        proj[:, (pair * heads + i) * 3 * DH + part * DH :][:, :DH] for i in range(heads)
    ]
    return pieces[0] if heads == 1 else jnp.concatenate(pieces, axis=1)


def forward_block(q_rows, k_all, v_masked, prev, width):
    raws, probs, total = [], [], None
    for i in range(width // DH):
        scores = dot_nt(pick(q_rows, i, width), k_all) + prev[i].astype(F32)
        raws.append(scores.astype(BF16))
        exponent = jnp.exp(scores - jnp.max(scores, axis=1, keepdims=True))
        scale = 1.0 / jnp.sum(exponent, axis=1, keepdims=True)
        prob = (exponent * scale).astype(BF16)
        probs.append(prob)
        out = dot_nn(prob, v_masked[i])
        total = out if total is None else total + out
    return raws, probs, total


def normalize(hidden):
    width = hidden.shape[1]
    center = hidden - jnp.sum(hidden, axis=1, keepdims=True) * (1.0 / width)
    inv_std = lax.rsqrt(jnp.sum(center * center, axis=1, keepdims=True) * (1.0 / width) + norm_eps)
    return center * inv_std, inv_std


def norm_back(scaled, xhat, inv_std):
    width = scaled.shape[1]
    mean_grad = jnp.sum(scaled, axis=1, keepdims=True) * (1.0 / width)
    mean_cross = jnp.sum(scaled * xhat, axis=1, keepdims=True) * (1.0 / width)
    return inv_std * (scaled - mean_grad - xhat * mean_cross)


def col_sum(value):
    return jnp.sum(value, axis=0, keepdims=True)


def middle_kernel(
    dims, tok_ref, att_ref, og_ref, w_ref, vec_ref, raw_in,
    out_ref, dh_ref, datt_ref, gw_ref, gvec_ref, raw_out,
    act_s, slope_s, bounce, in_sem, out_sem,
):
    cols, share, hw, fw = dims
    feat = vec_ref.shape[2]
    pairs, width = att_ref.shape[1], att_ref.shape[3]
    slots, rows_dev = bounce.shape[0], w_ref.shape[0]
    shard = w_ref.shape[2]
    cut = min(512, fw)
    me = lax.axis_index("col")

    takes = [pltpu.make_async_copy(raw_in.at[n], bounce.at[n], in_sem.at[n]) for n in range(slots)]
    puts = [pltpu.make_async_copy(bounce.at[n], raw_out.at[n], out_sem.at[n]) for n in range(slots)]
    for c in takes:
        c.start()

    def side(ref, i):
        return jnp.concatenate([ref[c, i : i + 1] for c in range(cols)], axis=1).astype(F32)

    def weight(c, a, b):
        return w_ref[:, c, :, a:b].reshape(rows_dev * shard, b - a)

    def put_weight(c, a, b, value):
        gw_ref[:, c, :, a:b] = value.astype(BF16).reshape(rows_dev, shard, b - a)

    own = pl.ds(pl.multiple_of(me * share, share), share)
    out_bias, gain1, shift1, ff2_bias, gain2, shift2 = (side(vec_ref, i) for i in range(6))
    tok = jnp.concatenate([tok_ref[c, own, :] for c in range(cols)], axis=1)

    hidden1 = tok.astype(F32) + out_bias
    for c in range(cols):
        for j in range(pairs):
            hidden1 = hidden1 + dot_nt(att_ref[c, j], weight(c, j * width, (j + 1) * width))
    xhat1, inv1 = normalize(hidden1)
    normed1 = xhat1 * gain1 + shift1
    low1 = normed1.astype(BF16)

    chunks = [(c, o) for c in range(cols) for o in range(0, fw, cut)]
    hidden2 = normed1 + ff2_bias
    for c, o in chunks:
        at = c * fw + o
        bias = jnp.concatenate([vec_ref[c, 6 + (o + i) // feat : 7 + (o + i) // feat] for i in range(0, cut, feat)], axis=1)
        inner = dot_nn(low1, weight(c, hw + o, hw + o + cut)) + bias.astype(F32)
        half = 0.5 + 0.5 * lax.erf(inner * root_half)
        act = (inner * half).astype(BF16)
        act_s[:, at : at + cut] = act
        slope_s[:, at : at + cut] = half + inner * inv_root_two_pi * jnp.exp(-0.5 * inner * inner)
        hidden2 = hidden2 + dot_nt(act, weight(c, hw + fw + o, hw + fw + o + cut))
    for n in range(slots):
        takes[n].wait()
        puts[n].start()
    xhat2, inv2 = normalize(hidden2)
    output = (xhat2 * gain2 + shift2).astype(BF16)

    og = jnp.concatenate([og_ref[c] for c in range(cols)], axis=1).astype(F32)
    d_hidden2 = norm_back(og * gain2, xhat2, inv2)
    low2 = d_hidden2.astype(BF16)
    rows = [None] * 6
    rows[4] = col_sum(og * xhat2)
    rows[5] = col_sum(og)
    rows[3] = col_sum(low2.astype(F32))
    low1_t = low1.T
    low2_t = low2.T
    d_normed1 = d_hidden2
    for c, o in chunks:
        at = c * fw + o
        d_act = dot_nn(low2, weight(c, hw + fw + o, hw + fw + o + cut))
        d_inner = (d_act * slope_s[:, at : at + cut]).astype(BF16)
        d_normed1 = d_normed1 + dot_nt(d_inner, weight(c, hw + o, hw + o + cut))
        put_weight(c, hw + o, hw + o + cut, dot_nn(low1_t, d_inner))
        put_weight(c, hw + fw + o, hw + fw + o + cut, dot_nn(low2_t, act_s[:, at : at + cut]))
        sums = col_sum(d_inner.astype(F32))
        for i in range(0, cut, feat):
            gvec_ref[c, 6 + (o + i) // feat : 7 + (o + i) // feat] = sums[:, i : i + feat]

    rows[1] = col_sum(d_normed1 * xhat1)
    rows[2] = col_sum(d_normed1)
    d_hidden1 = norm_back(d_normed1 * gain1, xhat1, inv1)
    low = d_hidden1.astype(BF16)
    rows[0] = col_sum(low.astype(F32))
    low_t = low.T
    spare = gvec_ref.shape[1] - 6 - fw // feat
    for c in range(cols):
        for j in range(pairs):
            put_weight(c, j * width, (j + 1) * width, dot_nn(low_t, att_ref[c, j]))
        datt_ref[c] = dot_nn(low, weight(c, 0, hw)).astype(BF16)
        span = slice(c * feat, (c + 1) * feat)
        out_ref[c] = output[:, span]
        dh_ref[c] = low[:, span]
        for i in range(6):
            gvec_ref[c, i : i + 1] = rows[i][:, span]
        if spare:
            gvec_ref[c, 6 + fw // feat :] = jnp.zeros((spare, feat), F32)
    for c in puts:
        c.wait()


def middle(tok, att, og, w, vec, raw):
    rows_dev, cols, shard, _ = w.shape
    feat = tok.shape[2]
    share = og.shape[1]
    hw = att.shape[1] * att.shape[3]
    fw = (w.shape[3] - hw) // 2
    slots = 8
    pieces = (slots, raw.shape[0] * raw.shape[1] // slots, raw.shape[2])
    vmem = pl.BlockSpec(memory_space=pltpu.VMEM)
    anywhere = pl.BlockSpec(memory_space=pl.ANY)
    results = pl.pallas_call(
        functools.partial(middle_kernel, (cols, share, hw, fw)),
        out_shape=[
            jax.ShapeDtypeStruct((cols, share, feat), BF16),
            jax.ShapeDtypeStruct((cols, share, feat), BF16),
            jax.ShapeDtypeStruct((cols, share, hw), BF16),
            jax.ShapeDtypeStruct(w.shape, BF16),
            jax.ShapeDtypeStruct(vec.shape, F32),
            jax.ShapeDtypeStruct(pieces, BF16),
        ],
        in_specs=[vmem] * 5 + [anywhere],
        out_specs=[vmem] * 5 + [anywhere],
        scratch_shapes=[
            pltpu.VMEM((share, cols * fw), BF16),
            pltpu.VMEM((share, cols * fw), F32),
            pltpu.VMEM(pieces, BF16),
            pltpu.SemaphoreType.DMA((slots,)),
            pltpu.SemaphoreType.DMA((slots,)),
        ],
        compiler_params=pltpu.CompilerParams(vmem_limit_bytes=60 << 20),
        name="middle",
    )(tok, att, og, w, vec, raw.reshape(pieces))
    return *results[:-1], results[-1].reshape(raw.shape)


MESH = pl.DeviceIdType.MESH


def chip_at(place, chips):
    place = lax.rem(place + 2 * chips, chips)
    return jnp.where(place < chips // 2, 2 * place, 2 * (chips - 1 - place) + 1)


def place_of(chip, chips):
    return jnp.where(lax.rem(chip, 2) == 0, chip // 2, chips - 1 - chip // 2)


class Spot:
    def __init__(self, devices_row, cols):
        self.cols = cols
        self.chips = devices_row // 2
        self.row = lax.axis_index("row")
        self.me = lax.axis_index("col")
        self.core = lax.rem(self.row, 2)
        self.place = place_of(self.row // 2, self.chips)
        self.partner = (self.row + 1 - 2 * self.core, self.me)

    def row_at(self, offset):
        return 2 * chip_at(self.place + offset, self.chips) + self.core

    def ring(self, way):
        return (self.row_at(1 if way == 0 else -1), self.me)

    def peer(self, j):
        return lax.rem(self.me + j + self.cols, self.cols)

    def col_peer(self, j):
        return (self.row, self.peer(j))


def greet(others):
    barrier = pltpu.get_barrier_semaphore()
    for other in others:
        pl.semaphore_signal(barrier, inc=1, device_id=other, device_id_type=MESH)
    pl.semaphore_wait(barrier, len(others))


def rcopy(src, dst, send, recv, to):
    return pltpu.make_async_remote_copy(
        src_ref=src, dst_ref=dst, send_sem=send, recv_sem=recv, device_id=to, device_id_type=MESH
    )


def cuts(weights):
    n = 2 if weights % 256 == 0 else 1
    return [pl.ds(i * (weights // n), weights // n) for i in range(n)]


def depth(chips, k, way):
    return chips // 2 if k == way else chips // 2 - 1


def front_kernel(
    dims, tok, wq, w_out, w_ff1, w_ff2, side0, side1, side2, side3, side4, side5, side6, og, bias, prev, raw, prob, tok_all, proj_all, wf_all, wq_all, vec_all, og_all, att_all,
    tok_s, wq_s, proj_s, q_s, k_s, v_s, att_s, wf, vec, wf_v,
    x_send, x_recv, q_send, q_recv, f_send, f_recv, p_send, p_recv, a_send, a_recv, l_sem,
):
    cols, rows_dev, seqs, heads, pairs, share, block = dims
    at = Spot(rows_dev, cols)
    chips, me, row = at.chips, at.me, at.row
    half_size = cols // 2
    width = heads * DH
    length = prev.shape[2]
    per = length // share
    turns = length // block
    in_share = share // block
    step = pl.program_id(0)
    steps = pairs * seqs * turns
    group = step // turns
    pos = lax.rem(step, turns)
    pair_now = group // seqs
    seq_now = lax.rem(group, seqs)
    turn = lax.rem(pos + lax.rem(me + 1, per) * in_share, turns)
    offs = [j for j in range(1, cols)]
    far = chips // 2
    pieces = cuts(wf.shape[1])
    kinds = ("tok", "tok2", "wf", "vec", "og")
    first = pl.ds(0, tok.shape[0] // 2)
    second = pl.ds(tok.shape[0] // 2, tok.shape[0] // 2)

    def half(k):
        mine = me // half_size
        first = mine if k == 0 else 1 - mine
        return pl.ds(first * half_size, half_size)

    def off(way, h):
        return -h if way == 0 else h

    def q_hop(way, h):
        r = at.row_at(off(way, h - 1))
        src = wq if h == 1 else wq_s.at[r]
        return rcopy(src, wq_s.at[r], q_send.at[way, h - 1], q_recv.at[way, h - 1], at.ring(way))

    def q_got(way, h):
        r = at.row_at(off(way, h))
        return rcopy(wq, wq_s.at[r], q_send.at[way, h - 1], q_recv.at[way, h - 1], at.ring(way))

    def q_pair(way, h, mine=True):
        r = at.row_at(off(way, h))
        src = wq if h == 0 else wq_s.at[r]
        if not mine:
            r = r + 1 - 2 * at.core
        return rcopy(src, wq_s.at[r], q_send.at[2 + way, h], q_recv.at[2 + way, h], at.partner)

    def f_hop(k, p, way, h):
        part = wf_v.at[at.row_at(off(way, h - 1)), half(k), :, pieces[p]]
        return rcopy(part, part, f_send.at[k, p, way, h - 1], f_recv.at[k, p, way, h - 1], at.ring(way))

    def f_got(k, p, way, h):
        part = wf_v.at[at.row_at(off(way, h)), half(k), :, pieces[p]]
        return rcopy(part, part, f_send.at[k, p, way, h - 1], f_recv.at[k, p, way, h - 1], at.ring(way))

    def f_pair(k, p, way, h, mine=True):
        r = at.row_at(off(way, h))
        if not mine:
            r = r + 1 - 2 * at.core
        part = wf_v.at[r, half(k), :, pieces[p]]
        return rcopy(part, part, p_send.at[k, p, way, h], p_recv.at[k, p, way, h], at.partner)

    def f_own(k, p):
        f_hop(k, p, 0, 1).start()
        f_hop(k, p, 1, 1).start()
        f_pair(k, p, 0, 0).start()

    def x_copy(kind, j):
        to = at.peer(j)
        src, dst = {
            "tok": (tok.at[first], tok_s.at[me, first]),
            "tok2": (tok.at[second], tok_s.at[me, second]),
            "wf": (wf, wf_v.at[row, me]),
            "vec": (vec, vec_all.at[me]),
            "og": (og.at[pl.ds(pl.multiple_of(to * share, share), share)], og_all.at[me]),
        }[kind]
        n = kinds.index(kind)
        return rcopy(src, dst, x_send.at[n, j - 1], x_recv.at[n, j - 1], at.col_peer(j))

    def x_got(kind, j):
        came = at.peer(-j)
        src, dst = {
            "tok": (tok.at[first], tok_s.at[came, first]),
            "tok2": (tok.at[second], tok_s.at[came, second]),
            "wf": (wf, wf_v.at[row, came]),
            "vec": (vec, vec_all.at[came]),
            "og": (og.at[pl.ds(0, share)], og_all.at[came]),
        }[kind]
        n = kinds.index(kind)
        return rcopy(src, dst, x_send.at[n, j - 1], x_recv.at[n, j - 1], at.col_peer(j))

    def locals_():
        own = pl.ds(pl.multiple_of(me * share, share), share)
        return [
            pltpu.make_async_copy(wf, wf_v.at[row, me], l_sem.at[0]),
            pltpu.make_async_copy(wq, wq_s.at[row], l_sem.at[1]),
            pltpu.make_async_copy(tok, tok_s.at[me], l_sem.at[2]),
            pltpu.make_async_copy(vec, vec_all.at[me], l_sem.at[3]),
            pltpu.make_async_copy(og.at[own], og_all.at[me], l_sem.at[4]),
        ]

    def saves():
        return [
            pltpu.make_async_copy(tok_s, tok_all, l_sem.at[0]),
            pltpu.make_async_copy(wq_s, wq_all, l_sem.at[1]),
            pltpu.make_async_copy(proj_s, proj_all, l_sem.at[2]),
        ]

    def handle(k, h, only=None):
        for p in range(len(pieces)) if only is None else only:
            for way in range(2):
                if h <= depth(chips, k, way):
                    f_got(k, p, way, h).wait_recv()
                    if h < depth(chips, k, way):
                        f_hop(k, p, way, h + 1).start()
                    f_pair(k, p, way, h).start()

    @pl.when(step == 0)
    def _():
        hw, fw = w_out.shape[1], w_ff1.shape[1]
        wf[:, :hw] = w_out[...]
        wf[:, hw : hw + fw] = w_ff1[...]
        wf[:, hw + fw :] = w_ff2[...]
        feat = vec.shape[1]
        vec[...] = jnp.zeros_like(vec)
        for i, ref in enumerate((side0, side1, side2, side3, side4, side5)):
            vec[i : i + 1, :] = ref[...].reshape(1, feat)
        long = side6[...].reshape(1, fw)
        for i in range(fw // feat):
            vec[6 + i : 7 + i, :] = long[:, i * feat : (i + 1) * feat]
        greet([at.ring(0), at.ring(1), at.partner] + [at.col_peer(j) for j in offs])
        q_hop(0, 1).start()
        q_hop(1, 1).start()
        for kind in ("wf", "tok", "tok2", "vec"):
            for j in offs:
                x_copy(kind, j).start()
        q_pair(0, 0).start()
        for c in locals_():
            c.start()
        for c in locals_():
            c.wait()
        if cols > 2:
            for j in offs:
                x_got("wf", j).wait_recv()
        for h in range(1, far + 1):
            for way in range(2):
                if h <= depth(chips, 0, way):
                    q_got(way, h).wait_recv()
                    if h < depth(chips, 0, way):
                        q_hop(way, h + 1).start()
                    q_pair(way, h).start()
            if h == 1:
                for p in range(len(pieces)):
                    f_own(0, p)
            if h == 2:
                if cols == 2:
                    for j in offs:
                        x_got("wf", j).wait_recv()
                for p in range(len(pieces)):
                    f_own(1, p)
            if h == 3:
                handle(0, 1)
        for j in offs:
            x_copy("og", j).start()
        handle(1, 1)
        for way in range(2):
            for h in range(0 if way == 0 else 1, depth(chips, 0, way) + 1):
                q_pair(way, h, mine=False).wait_recv()
        for j in offs:
            x_got("tok", j).wait_recv()
        rows = wq_s.shape[0] // cols
        chunk = min(512, tok.shape[0])

        def project(i, carry):
            span = pl.ds(pl.multiple_of(i * chunk, chunk), chunk)

            @pl.when(i == tok.shape[0] // chunk // 2)
            def _():
                for j in offs:
                    x_got("tok2", j).wait_recv()
                handle(0, 2)

            total = bias[...].reshape(1, -1).astype(F32)
            for c in range(cols):
                w = wq_s[c * rows : (c + 1) * rows].reshape(-1, wq_s.shape[2])
                total = total + dot_nn(tok_s[c, span, :], w)
            proj_s[span, :] = total.astype(BF16)
            return carry

        lax.fori_loop(0, tok.shape[0] // chunk, project, 0)
        handle(1, 2)

    @pl.when(pos == 0)
    def _():
        for pair in range(pairs):

            @pl.when(pair_now == pair)
            def _():
                proj = proj_s[pl.ds(pl.multiple_of(seq_now * length, length), length), :]
                q_s[...] = part_of(proj, pair, heads, 0) * jnp.asarray(0.125, BF16)
                k_s[...] = part_of(proj, pair, heads, 1)
                v = part_of(proj, pair, heads, 2)
                for i in range(heads):
                    v_s[i] = pick(v, i, width)

    def att_copy(g, t, to):
        i = lax.rem(me + 1 + t, per)
        j = g // seqs
        return rcopy(
            att_s.at[g, pl.ds(pl.multiple_of(i * share, share), share)],
            att_all.at[me, j],
            a_send.at[g, t],
            a_recv.at[j, me],
            (row, to),
        )

    def att_keep(g, t):
        i = lax.rem(me + 1 + t, per)
        return pltpu.make_async_copy(
            att_s.at[g, pl.ds(pl.multiple_of(i * share, share), share)], att_all.at[me, g // seqs], l_sem.at[3]
        )

    def att_to(g, t):
        return lax.rem(g, seqs) * per + lax.rem(me + 1 + t, per)

    def att_send(done):
        g = done // turns
        t = lax.rem(done, turns) // in_share
        to = att_to(g, t)

        @pl.when(to != me)
        def _():
            att_copy(g, t, to).start()

        @pl.when(to == me)
        def _():
            c = att_keep(g, t)
            c.start()
            c.wait()

    @pl.when((step > 0) & (lax.rem(step, in_share) == 0))
    def _():
        att_send(step - 1)

    at_step = {1: [(0, 3)], 2: [(1, 3)], 3: [(0, 4)], 5: [(1, 4)], 7: []}
    for h in range(5, far + 1):
        at_step[7] += [(0, h), (1, h)]
    for n, todo in at_step.items():

        @pl.when(step == n * steps // 8)
        def _(todo=todo):
            for k, h in todo:
                handle(k, h)

    @pl.when(step == 1)
    def _():
        for c in saves():
            c.start()

    rows_now = pl.ds(pl.multiple_of(turn * block, block), block)
    raws, probs, out = forward_block(
        q_s[rows_now, :], k_s[...], [v_s[i] for i in range(heads)], [prev[i] for i in range(heads)], width
    )
    for i in range(heads):
        raw[i] = raws[i]
        prob[i] = probs[i]
    att_s[group, rows_now, :] = out.astype(BF16)

    @pl.when(step == steps - 1)
    def _():
        att_send(step)
        for c in saves():
            c.wait()
        for j in offs:
            for kind in kinds:
                x_copy(kind, j).wait_send()
                if kind in ("vec", "og"):
                    x_got(kind, j).wait_recv()
        for way in range(2):
            for h in range(1, depth(chips, 0, way) + 1):
                q_hop(way, h).wait_send()
            for h in range(0 if way == 0 else 1, depth(chips, 0, way) + 1):
                q_pair(way, h).wait_send()
            for k in range(2):
                for p in range(len(pieces)):
                    for h in range(1, depth(chips, k, way) + 1):
                        f_hop(k, p, way, h).wait_send()
                    for h in range(0 if way == 0 else 1, depth(chips, k, way) + 1):
                        f_pair(k, p, way, h).wait_send()
                        f_pair(k, p, way, h, mine=False).wait_recv()
        keep = pltpu.make_async_copy(wf_v, wf_all, l_sem.at[4])
        keep.start()
        for g in range(pairs * seqs):
            for t in range(per):
                to = att_to(g, t)

                @pl.when(to != me)
                def _():
                    att_copy(g, t, to).wait_send()

        for p in range(pairs):
            for j in offs:
                came = at.peer(j)
                rcopy(
                    att_s.at[0, pl.ds(0, share)], att_all.at[came, p], a_send.at[0, 0], a_recv.at[p, came], at.col_peer(j)
                ).wait_recv()
        keep.wait()


def front(cols, rows_dev, seqs, head_count, tok, wq, w_out, w_ff1, w_ff2, sides, og, bias, prev):
    heads = min(2, head_count)
    pairs = head_count // heads
    total, feat = tok.shape
    share = total // cols
    length = prev.shape[-1]
    width = heads * DH
    block = min(256, share)
    turns = length // block
    per = length // share
    in_share = share // block
    chips = rows_dev // 2
    far = chips // 2
    groups = pairs * seqs
    shard = wq.shape[0]
    weights = w_out.shape[1] + 2 * w_ff1.shape[1]
    n = len(cuts(weights))

    def stream(s):
        g = s // turns
        turn = lax.rem(lax.rem(s, turns) + lax.rem(lax.axis_index("col") + 1, per) * in_share, turns)
        return (lax.rem(g, seqs) * pairs + g // seqs, turn, 0)

    def whole(x):
        n = x.ndim
        return pl.BlockSpec(x.shape, lambda s: (0,) * n, pipeline_mode=pl.Buffered(1))

    blocks = pl.BlockSpec((heads, block, length), stream)
    anywhere = pl.BlockSpec(memory_space=pl.ANY)
    dma = pltpu.SemaphoreType.DMA
    shapes = [
        (cols, total, feat),
        (total, wq.shape[1]),
        (rows_dev, cols, shard, weights),
        (rows_dev,) + wq.shape,
        (cols, 16, feat),
        (cols, share, feat),
        (cols, pairs, share, width),
    ]
    return pl.pallas_call(
        functools.partial(front_kernel, (cols, rows_dev, seqs, heads, pairs, share, block)),
        grid=(groups * turns,),
        in_specs=[whole(x) for x in (tok, wq, w_out, w_ff1, w_ff2, *sides, og, bias)] + [blocks],
        out_specs=[blocks, blocks] + [anywhere] * 7,
        out_shape=[jax.ShapeDtypeStruct(prev.shape, BF16)] * 2 + [jax.ShapeDtypeStruct(s, BF16) for s in shapes],
        scratch_shapes=[
            pltpu.VMEM((cols, total, feat), BF16),
            pltpu.VMEM((rows_dev,) + wq.shape, BF16),
            pltpu.VMEM((total, wq.shape[1]), BF16),
            pltpu.VMEM((length, width), BF16),
            pltpu.VMEM((length, width), BF16),
            pltpu.VMEM((heads, length, width), BF16),
            pltpu.VMEM((groups, length, width), BF16),
            pltpu.VMEM((shard, weights), BF16),
            pltpu.VMEM((16, feat), BF16),
            pltpu.VMEM((rows_dev, cols, shard, weights), BF16),
            dma((5, cols - 1)),
            dma((5, cols - 1)),
            dma((4, far + 1)),
            dma((4, far + 1)),
            dma((2, n, 2, far)),
            dma((2, n, 2, far)),
            dma((2, n, 2, far + 1)),
            dma((2, n, 2, far + 1)),
            dma((groups, per)),
            dma((pairs, cols)),
            dma((5,)),
        ],
        compiler_params=pltpu.CompilerParams(
            collective_id=1, has_side_effects=True, vmem_limit_bytes=60 << 20
        ),
        name="front",
    )(tok, wq, w_out, w_ff1, w_ff2, *sides, og, bias, prev)


def back_kernel(
    dims, proj, wq, tok, datt, outp, dh, gvec, gw, prob, cot,
    pg, out_all, ig, gwo, gqo, gvo,
    datt_s, out_s, dh_s, q_s, k_s, v_s, dq_s, dk_s, dv_s, dp_s,
    own_s, part_s, run_s, run_r, fin_s, fin_r,
    gq_s, gq_p, gq_t, gq_r, ip_s, xi_s, xi_r, vp_s, vs_s, vx_s, vr_s,
    x_send, x_recv, p_send, p_recv, r_send, r_recv, g_send, g_recv, v_send, v_recv, l_sem,
):
    cols, rows_dev, seqs, heads, pairs, share, block = dims
    at = Spot(rows_dev, cols)
    chips, me, core = at.chips, at.me, at.core
    chip = at.row // 2
    half_size = cols // 2
    width = heads * DH
    wide = 3 * width
    length = prob.shape[2]
    per = length // share
    turns = length // block
    in_share = share // block
    shard = gw.shape[3]
    pieces = cuts(gw.shape[4])
    step = pl.program_id(0)
    steps = pairs * seqs * turns
    group = step // turns
    pos = lax.rem(step, turns)
    pair_now = group // seqs
    seq_now = lax.rem(group, seqs)
    turn = lax.rem(pos + lax.rem(me, per) * in_share, turns)
    offs = list(range(1, cols))
    hops = list(range(1, chips))
    far = chips // 2
    total_rows = seqs * length

    def half(k):
        mine = me // half_size
        first = mine if k == 0 else 1 - mine
        return pl.ds(first * half_size, half_size)

    def chip_of(o):
        return chip_at(at.place + o, chips)

    def to_chip(o):
        return (2 * chip_of(o) + core, me)

    def x_copy(kind, j):
        to = at.peer(j)
        src, dst = [
            lambda: (datt.at[to], datt_s.at[me]),
            lambda: (outp.at[to], out_s.at[me]),
            lambda: (dh.at[to], dh_s.at[me]),
            lambda: (fin_s.at[to], fin_r.at[me]),
            lambda: (xi_s.at[j - 1], xi_r.at[j - 1]),
            lambda: (vs_s.at[to], vx_s.at[me]),
        ][kind]()
        return rcopy(src, dst, x_send.at[kind, j - 1], x_recv.at[kind, j - 1], at.col_peer(j))

    def x_got(kind, j):
        came = at.peer(-j)
        src, dst = [
            lambda: (datt.at[came], datt_s.at[came]),
            lambda: (outp.at[came], out_s.at[came]),
            lambda: (dh.at[came], dh_s.at[came]),
            lambda: (fin_s.at[came], fin_r.at[came]),
            lambda: (xi_s.at[j - 1], xi_r.at[j - 1]),
            lambda: (vs_s.at[came], vx_s.at[came]),
        ][kind]()
        return rcopy(src, dst, x_send.at[kind, j - 1], x_recv.at[kind, j - 1], at.col_peer(j))

    def part_copy(o):
        c = chip_of(o)
        return rcopy(gw.at[c, 1 - core], part_s.at[c], p_send.at[o % chips], p_recv.at[o % chips], at.partner)

    def own_load():
        return pltpu.make_async_copy(gw.at[:, core], own_s, l_sem.at[0])

    def locals_():
        return [
            pltpu.make_async_copy(datt.at[me], datt_s.at[me], l_sem.at[1]),
            pltpu.make_async_copy(outp.at[me], out_s.at[me], l_sem.at[2]),
            pltpu.make_async_copy(dh.at[me], dh_s.at[me], l_sem.at[3]),
        ]

    def run_copy(k, p, way, t):
        here = (k, p, way, t - 1)
        return rcopy(run_s.at[here], run_r.at[here], r_send.at[here], r_recv.at[here], at.ring(way))

    waited = set()

    def chip_sum(k, p, o):
        if o % chips not in waited:
            waited.add(o % chips)
            part_copy(o).wait_recv()
        c = chip_of(o)
        return own_s[c, half(k), :, pieces[p]].astype(F32) + part_s[c, half(k), :, pieces[p]].astype(F32)

    def run_step(k, p, t):
        for way in range(2):
            o = depth(chips, k, way) + 1 - t
            if o < 1:
                continue
            value = chip_sum(k, p, o if way == 0 else -o)
            if t > 1:
                run_copy(k, p, way, t - 1).wait_recv()
                value = value + run_r[k, p, way, t - 2].astype(F32)
            run_s[k, p, way, t - 1] = value.astype(BF16)
            run_copy(k, p, way, t).start()

    def run_last(k, p):
        value = chip_sum(k, p, 0)
        for way in range(2):
            d = depth(chips, k, way)
            run_copy(k, p, way, d).wait_recv()
            value = value + run_r[k, p, way, d - 1].astype(F32)
        fin_s[half(k), :, pieces[p]] = value.astype(BF16)

    streams = [(k, p) for p in range(len(pieces)) for k in range(2)]

    def run_round(t, only=None):
        for n, (k, p) in enumerate(streams):
            if only is None or n in only:
                run_step(k, p, t)

    def v_pair():
        return rcopy(gvec, vp_s, v_send.at[0], v_recv.at[0], at.partner)

    def v_chip(o):
        return rcopy(vr_s.at[chip], vr_s.at[chip], v_send.at[o], v_recv.at[o], to_chip(o))

    def v_chip_got(o):
        c = chip_of(-o)
        return rcopy(vr_s.at[c], vr_s.at[c], v_send.at[o], v_recv.at[o], to_chip(o))

    def v_second():
        v_pair().wait_recv()
        vs_s[...] = gvec[...] + vp_s[...]
        for j in offs:
            x_copy(5, j).start()

    def v_third():
        value = vs_s[me]
        for j in offs:
            x_got(5, j).wait_recv()
            value = value + vx_s[at.peer(-j)]
        vr_s[chip] = value
        for o in hops:
            v_chip(o).start()

    def g_pair(j):
        return rcopy(gq_s.at[:, 1 - core], gq_p.at[j], g_send.at[j, 0], g_recv.at[j, 0], at.partner)

    def g_chip(j, o):
        return rcopy(gq_t.at[j, chip_of(o)], gq_r.at[j, chip], g_send.at[j, o], g_recv.at[j, o], to_chip(o))

    def g_chip_got(j, o):
        return rcopy(gq_t.at[j, 0], gq_r.at[j, chip_of(-o)], g_send.at[j, o], g_recv.at[j, o], to_chip(o))

    def g_weight(j):
        slots = chips // cols
        for c in range(cols):
            value = dot_tn(tok[c], dp_s[...]).astype(BF16)
            gq_s[c * slots : (c + 1) * slots, :, :shard, :] = value.reshape(slots, 2, shard, wide)
        sums = col_sum(dp_s[...].astype(F32))
        line = lax.broadcasted_iota(jnp.int32, (16, wide), 0)
        low = jnp.where(line == 0, jnp.broadcast_to(sums, (16, wide)), 0.0).astype(BF16)
        gq_s[:, :, shard:, :] = jnp.broadcast_to(low[None, None], (chips, 2, 16, wide))
        g_pair(j).start()

    def g_pass(j):
        g_pair(j).wait_recv()
        gq_t[j] = (gq_s[:, core].astype(F32) + gq_p[j].astype(F32)).astype(BF16)
        gq_r[j, chip] = gq_t[j, chip]
        for o in hops:
            g_chip(j, o).start()

    def g_last(j):
        for o in hops:
            g_chip_got(j, o).wait_recv()
        value = gq_r[j, 0].astype(F32)
        for c in range(1, chips):
            value = value + gq_r[j, c].astype(F32)
        gqo[:, j * wide : (j + 1) * wide] = value

    chunk = min(512, total_rows)

    def input_part(j, n):
        slots = rows_dev // cols
        w = wq[pl.ds(at.peer(n) * slots, slots), :, j * wide : (j + 1) * wide].reshape(slots * shard, wide)

        def go(i, carry):
            span = pl.ds(pl.multiple_of(i * chunk, chunk), chunk)
            value = dot_nt(dp_s[span, :], w)
            if j > 0:
                value = value + ip_s[n, span, :]
            if j < pairs - 1:
                ip_s[n, span, :] = value
            elif n > 0:
                xi_s[n - 1, span, :] = value.astype(BF16)
            else:
                ip_s[0, span, :] = value
            return carry

        lax.fori_loop(0, total_rows // chunk, go, 0)

    @pl.when(step == 0)
    def _():
        greet(
            [at.ring(0), at.ring(1), at.partner]
            + [at.col_peer(j) for j in offs]
            + [to_chip(o) for o in hops if o not in (1, chips - 1)]
        )
        for j in offs:
            x_copy(0, j).start()
        own_load().start()
        v_pair().start()
        order = [far] + [s * o for o in range(far - 1, 0, -1) for s in (1, -1)] + [0]
        for o in order:
            part_copy(o).start()
        for c in locals_():
            c.start()
        for c in locals_():
            c.wait()
        if seqs > 1:
            for j in offs:
                x_got(0, j).wait_recv()

    if seqs == 1:

        @pl.when(step == in_share)
        def _():
            for j in offs:
                x_got(0, j).wait_recv()

    @pl.when(pos == 0)
    def _():
        for pair in range(pairs):

            @pl.when(pair_now == pair)
            def _():
                here = proj[pl.ds(pl.multiple_of(seq_now * length, length), length), :]
                q_s[...] = part_of(here, pair, heads, 0) * jnp.asarray(0.125, BF16)
                k = part_of(here, pair, heads, 1)
                for i in range(heads):
                    k_s[i] = pick(k, i, width)
                v_s[...] = part_of(here, pair, heads, 2)

        dk_s[...] = jnp.zeros_like(dk_s)
        dv_s[...] = jnp.zeros_like(dv_s)

    jobs = {
        0: [lambda: own_load().wait(), lambda: run_round(1)],
        1: [v_second] + [lambda kind=kind, j=j: x_copy(kind, j).start() for kind in (1, 2) for j in offs],
        2: [lambda: run_round(2, (0, 1))],
        3: [lambda: run_round(2, (2,)), v_third],
        4: [lambda: run_round(2, (3,)), lambda: run_round(3, (0,))],
        5: [lambda: run_round(3, (1,))],
        6: [lambda: run_round(3, (2, 3))],
        7: [lambda: run_round(4, (0,))],
    }

    def spot(n):
        return (n * steps) // 8

    for n, todo in jobs.items():

        @pl.when(step == spot(n))
        def _(todo=todo):
            for job in todo:
                job()

    @pl.when((step == steps // pairs) & (pairs > 1))
    def _():
        if pairs > 1:
            g_pass(0)

    rows_now = pl.ds(pl.multiple_of(turn * block, block), block)
    q_rows = q_s[rows_now, :]
    source = seq_now * per + turn // in_share
    inside = pl.ds(pl.multiple_of(lax.rem(turn, in_share) * block, block), block)
    dq = dk = dv = None
    for pair in range(pairs):

        @pl.when(pair_now == pair)
        def _():
            dq = dk = dv = None
            d_rows = datt_s[source, inside, pair * width : (pair + 1) * width]
            for i in range(heads):
                d_one = pick(d_rows, i, width)
                d_probs = dot_nt(d_one, v_s[...])
                p = prob[i]
                p_wide = p.astype(F32)
                delta = jnp.sum(d_probs * p_wide, axis=1, keepdims=True)
                low = (p_wide * (d_probs - delta) + cot[i].astype(F32)).astype(BF16)
                pg[i] = low
                a = dot_nn(low, k_s[i])
                b = dot_tn(pick(q_rows, i, width), low)
                c = dot_tn(d_one, p)
                dq = a if dq is None else dq + a
                dk = b if dk is None else dk + b
                dv = c if dv is None else dv + c
            dq_s[rows_now, :] = (dq * 0.125).astype(BF16)
            dk_s[...] += dk
            dv_s[...] += dv

    @pl.when(pos == turns - 1)
    def _():
        parts = [dq_s[...], dk_s[...].T.astype(BF16), dv_s[...].T.astype(BF16)]
        here = pl.ds(pl.multiple_of(seq_now * length, length), length)
        for i in range(heads):
            dp_s[here, i * 3 * DH : (i + 1) * 3 * DH] = jnp.concatenate([p[:, i * DH : (i + 1) * DH] for p in parts], axis=1)

    for j in range(pairs - 1):

        @pl.when(step == (j + 1) * (steps // pairs) - 1)
        def _():
            g_weight(j)
            for n in range(cols):
                input_part(j, n)

    @pl.when(step == steps - 1)
    def _():
        last = pairs - 1
        for j in offs:
            input_part(last, j)
            x_copy(4, j).start()
        if pairs > 1:
            g_pair(last - 1).wait_send()
        run_round(4, (1, 2, 3))
        g_weight(last)
        for t in range(5, far + 1):
            run_round(t)
        input_part(last, 0)
        g_pass(last)
        for j in offs:
            x_got(1, j).wait_recv()
            x_got(2, j).wait_recv()
        keep = pltpu.make_async_copy(out_s, out_all, l_sem.at[1])
        keep.start()
        for k, p in streams:
            run_last(k, p)
        for j in offs:
            x_copy(3, j).start()
        for o in hops:
            v_chip_got(o).wait_recv()
        value = vr_s[0]
        for c in range(1, chips):
            value = value + vr_s[c]
        gvo[...] = value
        for j in range(pairs):
            g_last(j)
        for j in offs:
            x_got(4, j).wait_recv()

        def finish(i, carry):
            c = i // (share // min(share, chunk))
            rows = min(share, chunk)
            inner = pl.ds(pl.multiple_of(lax.rem(i, share // rows) * rows, rows), rows)
            span = pl.ds(pl.multiple_of(i * rows, rows), rows)
            value = ip_s[0, span, :] + dh_s[c, inner, :].astype(F32)
            for j in offs:
                value = value + xi_r[j - 1, span, :].astype(F32)
            ig[span, :] = value.astype(BF16)
            return carry

        lax.fori_loop(0, total_rows // min(share, chunk), finish, 0)
        value = fin_s[me].astype(F32)
        for j in offs:
            x_got(3, j).wait_recv()
            value = value + fin_r[at.peer(-j)].astype(F32)
        gwo[...] = value
        keep.wait()
        for kind in range(6):
            for j in offs:
                x_copy(kind, j).wait_send()
        for o in range(chips):
            part_copy(o).wait_send()
        for k in range(2):
            for way in range(2):
                for t in range(1, depth(chips, k, way) + 1):
                    for p in range(len(pieces)):
                        run_copy(k, p, way, t).wait_send()
        v_pair().wait_send()
        for o in hops:
            v_chip(o).wait_send()
        g_pair(last).wait_send()
        for j in range(pairs):
            for o in hops:
                g_chip(j, o).wait_send()


def back(cols, rows_dev, seqs, head_count, proj, wq, tok, datt, outp, dh, gvec, gw, prob, cot):
    heads = min(2, head_count)
    pairs = head_count // heads
    _, total, feat = tok.shape
    share = total // cols
    length = prob.shape[-1]
    width = heads * DH
    wide = 3 * width
    block = min(256, share)
    turns = length // block
    per = length // share
    in_share = share // block
    chips = rows_dev // 2
    far = chips // 2
    shard, weights = gw.shape[2:]
    half_size = cols // 2
    n = len(cuts(weights))
    gw = gw.reshape(chips, 2, cols, shard, weights)

    def stream(s):
        g = s // turns
        turn = lax.rem(lax.rem(s, turns) + lax.rem(lax.axis_index("col"), per) * in_share, turns)
        return (lax.rem(g, seqs) * pairs + g // seqs, turn, 0)

    def whole(shape):
        n = len(shape)
        return pl.BlockSpec(shape, lambda s: (0,) * n, pipeline_mode=pl.Buffered(1))

    blocks = pl.BlockSpec((heads, block, length), stream)
    anywhere = pl.BlockSpec(memory_space=pl.ANY)
    dma = pltpu.SemaphoreType.DMA
    outs = [
        jax.ShapeDtypeStruct(prob.shape, BF16),
        jax.ShapeDtypeStruct((cols, share, feat), BF16),
        jax.ShapeDtypeStruct((total, feat), BF16),
        jax.ShapeDtypeStruct((shard, weights), F32),
        jax.ShapeDtypeStruct((shard + 16, wq.shape[2]), F32),
        jax.ShapeDtypeStruct(gvec.shape[1:], F32),
    ]
    return pl.pallas_call(
        functools.partial(back_kernel, (cols, rows_dev, seqs, heads, pairs, share, block)),
        grid=(pairs * seqs * turns,),
        in_specs=[whole(x.shape) for x in (proj, wq, tok, datt, outp, dh, gvec)] + [anywhere, blocks, blocks],
        out_specs=[blocks, anywhere] + [whole(o.shape) for o in outs[2:]],
        out_shape=outs,
        scratch_shapes=[
            pltpu.VMEM(datt.shape, BF16),
            pltpu.VMEM(outp.shape, BF16),
            pltpu.VMEM(dh.shape, BF16),
            pltpu.VMEM((length, width), BF16),
            pltpu.VMEM((heads, length, width), BF16),
            pltpu.VMEM((length, width), BF16),
            pltpu.VMEM((length, width), BF16),
            pltpu.VMEM((width, length), F32),
            pltpu.VMEM((width, length), F32),
            pltpu.VMEM((total, wide), BF16),
            pltpu.VMEM((chips, cols, shard, weights), BF16),
            pltpu.VMEM((chips, cols, shard, weights), BF16),
            pltpu.VMEM((2, n, 2, far, half_size, shard, weights // n), BF16),
            pltpu.VMEM((2, n, 2, far, half_size, shard, weights // n), BF16),
            pltpu.VMEM((cols, shard, weights), BF16),
            pltpu.VMEM((cols, shard, weights), BF16),
            pltpu.VMEM((chips, 2, shard + 16, wide), BF16),
            pltpu.VMEM((pairs, chips, shard + 16, wide), BF16),
            pltpu.VMEM((pairs, chips, shard + 16, wide), BF16),
            pltpu.VMEM((pairs, chips, shard + 16, wide), BF16),
            pltpu.VMEM((cols if pairs > 1 else 1, total, feat), F32),
            pltpu.VMEM((cols - 1, total, feat), BF16),
            pltpu.VMEM((cols - 1, total, feat), BF16),
            pltpu.VMEM(gvec.shape, F32),
            pltpu.VMEM(gvec.shape, F32),
            pltpu.VMEM(gvec.shape, F32),
            pltpu.VMEM((chips,) + gvec.shape[1:], F32),
            dma((6, cols - 1)),
            dma((6, cols - 1)),
            dma((chips,)),
            dma((chips,)),
            dma((2, n, 2, far)),
            dma((2, n, 2, far)),
            dma((pairs, chips)),
            dma((pairs, chips)),
            dma((chips,)),
            dma((chips,)),
            dma((4,)),
        ],
        compiler_params=pltpu.CompilerParams(
            collective_id=2, has_side_effects=True, vmem_limit_bytes=62 << 20
        ),
        name="back",
    )(proj, wq, tok, datt, outp, dh, gvec, gw, prob, cot)


def finish_kernel(cols, pg_in, out_in, ig_in, gw, gq, gv, pg, out, ig, wq, bq, wo, bo, n1g, n1s, w1, b1, w2, b2, n2g, n2s, bounce, in_sem, out_sem):
    slots = bounce.shape[0]
    takes = [pltpu.make_async_copy(pg_in.at[n], bounce.at[n], in_sem.at[n]) for n in range(slots)]
    puts = [pltpu.make_async_copy(bounce.at[n], pg.at[n], out_sem.at[n]) for n in range(slots)]
    for c in takes:
        c.start()
    shard = wq.shape[0]
    hw, fw = wo.shape[1], w1.shape[1]
    feat = out.shape[1]
    for c in range(cols):
        out[c * out_in.shape[1] : (c + 1) * out_in.shape[1], :] = out_in[c]
    ig[...] = ig_in[...]
    for n in range(slots // 2):
        takes[n].wait()
        puts[n].start()
    wq[...] = gq[:shard]
    bq[...] = gq[shard : shard + 1].reshape(-1)
    wo[...] = gw[:, :hw]
    w1[...] = gw[:, hw : hw + fw]
    w2[...] = gw[:, hw + fw :]
    for i, ref in enumerate((bo, n1g, n1s, b2, n2g, n2s)):
        ref[...] = gv[i : i + 1].reshape(-1)
    b1[...] = jnp.concatenate([gv[6 + i : 7 + i] for i in range(fw // feat)], axis=1).reshape(-1)
    for n in range(slots // 2, slots):
        takes[n].wait()
        puts[n].start()
    for c in puts:
        c.wait()


def finish(cols, pg, out, ig, gw, gq, gv, hw, fw):
    slots = 8
    pieces = (slots, pg.shape[0] * pg.shape[1] // slots, pg.shape[2])
    total, feat = ig.shape
    shard = gw.shape[0]
    vmem = pl.BlockSpec(memory_space=pltpu.VMEM)
    anywhere = pl.BlockSpec(memory_space=pl.ANY)

    def f32(*shape):
        return jax.ShapeDtypeStruct(shape, F32)

    outs = [
        jax.ShapeDtypeStruct(pieces, BF16),
        jax.ShapeDtypeStruct(ig.shape, BF16),
        jax.ShapeDtypeStruct(ig.shape, BF16),
        f32(shard, gq.shape[1]),
        f32(gq.shape[1]),
        f32(shard, hw),
        f32(feat),
        f32(feat),
        f32(feat),
        f32(shard, fw),
        f32(fw),
        f32(shard, fw),
        f32(feat),
        f32(feat),
        f32(feat),
    ]
    return pl.pallas_call(
        functools.partial(finish_kernel, cols),
        out_shape=outs,
        in_specs=[anywhere] + [vmem] * 5,
        out_specs=[anywhere] + [vmem] * 14,
        scratch_shapes=[
            pltpu.VMEM(pieces, BF16),
            pltpu.SemaphoreType.DMA((slots,)),
            pltpu.SemaphoreType.DMA((slots,)),
        ],
        compiler_params=pltpu.CompilerParams(vmem_limit_bytes=60 << 20),
        name="finish",
    )(pg.reshape(pieces), out, ig, gw, gq, gv)


def per_device(
    cols,
    row_count,
    tokens,
    prev_logits,
    qkv_weight,
    qkv_bias,
    out_weight,
    out_bias,
    norm1_gain,
    norm1_shift,
    ff1_weight,
    ff1_bias,
    ff2_weight,
    ff2_bias,
    norm2_gain,
    norm2_shift,
    out_grad,
    logit_grad,
):
    seqs, head_count, length, _ = prev_logits.shape
    total, feat = tokens.shape
    share = total // cols
    rows = min(256, length)
    rows_dev = row_count
    hidden = ff1_weight.shape[1]
    sides = (out_bias, norm1_gain, norm1_shift, ff2_bias, norm2_gain, norm2_shift, ff1_bias)
    prev = prev_logits.reshape(seqs * head_count, length, length)
    cot = logit_grad.reshape(seqs * head_count, length, length)
    raw, prob, tok_all, proj, wf_all, wq_all, vec_all, og_all, att_all = front(
        cols, rows_dev, seqs, head_count, tokens, qkv_weight, out_weight.T, ff1_weight, ff2_weight.T, sides, out_grad, qkv_bias, prev
    )
    out, dh, datt, gw, gvec, raw = middle(tok_all, att_all, og_all, wf_all, vec_all, raw)

    prev_grad, output, input_grad, gw, gq, gv = back(
        cols, rows_dev, seqs, head_count, proj, wq_all, tok_all, datt, out, dh, gvec, gw, prob, cot
    )
    prev_grad, output, input_grad, *rest = finish(
        cols, prev_grad, output, input_grad, gw, gq, gv, out_weight.shape[0], hidden
    )
    rest[2] = rest[2].T
    rest[8] = rest[8].T
    return output, raw.reshape(prev_logits.shape), input_grad, prev_grad.reshape(prev_logits.shape), *rest


def solution(mesh):
    in_specs = (
        P("row", "col"),
        P("row", "col", None, None),
        P("row", "col"),
        P("col"),
        P("col", "row"),
        P("col"),
        P("col"),
        P("col"),
        P("row", "col"),
        P("col"),
        P("col", "row"),
        P("col"),
        P("col"),
        P("col"),
        P("row", "col"),
        P("row", "col", None, None),
    )
    out_specs = (
        P("row", "col"),
        P("row", "col", None, None),
        P("row", "col"),
        P("row", "col", None, None),
        P("row", "col"),
        P("col"),
        P("col", "row"),
        P("col"),
        P("col"),
        P("col"),
        P("row", "col"),
        P("col"),
        P("col", "row"),
        P("col"),
        P("col"),
        P("col"),
    )
    return jax.shard_map(
        functools.partial(per_device, mesh.shape["col"], mesh.shape["row"]),
        mesh=mesh,
        in_specs=in_specs,
        out_specs=out_specs,
        check_vma=False,
    )
```

time: 419 us -> 128 us (0.31)
  waiting for transfers between devices: 166 us -> 0 us
  blocking collectives: 137 us -> 0 us
  Pallas kernels: 49.6 us -> 126 us
  local copies, waits for them, and re-layouts: 15.7 us -> 0 us
  starting transfers between devices: 14.5 us -> 0 us
  between operations: 14.4 us -> 0.86 us
  other arithmetic: 11.4 us -> 0 us
  matrix products: 9.3 us -> 0 us
    reduce_scatter x3 -> x0, waiting for transfers between devices: 76.8 us -> none  [the longest x1 76.8 us: per_device(): lax.psum_scatter(gw.astype(F32), 'row', scatter_dimension=1, tiled=True)]
    pallas_call x3 -> x4, Pallas kernels: 49.6 us -> 126 us  [the longest x1 50.6 us: back(): pl.pallas_call(functools.partial(back_kernel, (cols, rows_dev, seqs, head...]
    all_gather x3 -> x0, waiting for transfers between devices: 66.2 us -> none  [the longest x1 46.3 us: per_device(): lax.all_gather(mixed, 'row', axis=0, tiled=True)]
    psum x1 -> x0, blocking collectives: 60.6 us -> none  [per_device(): vec_sum, qkv_bias_grad = lax.psum((vec_sum, qkv_bias_grad), 'row')]
    all_gather x3 -> x0, blocking collectives: 41.1 us -> none  [the longest x1 21.3 us: per_device(): wide_qkv = lax.all_gather(qkv_weight, 'row', axis=0, tiled=True)]
    unnamed x1 -> x0, blocking collectives: 23.6 us -> none
    all_to_all x4 -> x0, starting transfers between devices: 14.3 us -> none  [the longest x2 7.14 us: to_rows(): return lax.all_to_all(x, 'col', split_axis=0, concat_axis=1, tiled=True)]
    unnamed x8 -> x0, waiting for transfers between devices: 11.7 us -> none
  transfers between devices with their start and end apart: 11 -> 0, of which waited for: 5 -> 0; matrix products, arithmetic and copies ran while one was open for 6% -> 0% of each run, Pallas kernels for 8% -> 0%
where the time goes in v2:
time: 128 us; the launch traced here: 127 us
  Pallas kernels  126 us (98%)
    pallas_call x1, Pallas kernels, back(): pl.pallas_call(functools.partial(back_kernel, (cols, rows_dev, seqs, head...  50.6 us
    pallas_call x1, Pallas kernels, front(): pl.pallas_call(functools.partial(front_kernel, (cols, rows_dev, seqs, hea...  50.1 us
    pallas_call x1, Pallas kernels, middle(): pl.pallas_call(functools.partial(middle_kernel, (cols, share, hw, fw)), o...  16.2 us
    pallas_call x1, Pallas kernels, finish(): pl.pallas_call(functools.partial(finish_kernel, cols), out_shape=outs, in...  8.88 us

profile of v2, /device:TPU:0, one launch (start us, length us, event | category | flops | bytes accessed | tf_op | source)
XLA Modules:
  0.0 126.6 jit_solution(7938735675810048369)
XLA Ops:
  0.7 50.1 %front.1 = (bf16[4,1024,1024]{2,1,0:T(8,128)(2,1)}, bf16[4,1024,1024]{2,1,0:T(8,128)(2,1)}, bf16[2,1024,256]{2,1,0:T(8,128)(2,1)}, bf16[1024,768]{1,0:T(8,128)(2...) custom-call(bf16[1024,256]{1,0:T(8,128)(2,1)} %tok.1, ...), custom_call_target="tpu_custom_call" | custom-call | tf_op jit(solution)/shard_map/front/pallas_call | solution.py:624
  50.8 16.2 %middle.1 = (bf16[2,512,256]{2,1,0:T(8,128)(2,1)}, bf16[2,512,256]{2,1,0:T(8,128)(2,1)}, bf16[2,512,256]{2,1,0:T(8,128)(2,1)}, bf16[16,2,32,2304]{3,2,1,0:T(8,12...) custom-call(bf16[2,1024,256]{2,1,0:T(8,128)(2,1)} %get-tuple-element.54.tok_ref.tok, ...), custom_call_target="tpu_custom_call" | custom-call | tf_op jit(solution)/shard_map/middle/pallas_call | solution.py:189
  67.0 50.6 %back.1 = (bf16[4,1024,1024]{2,1,0:T(8,128)(2,1)}, bf16[2,512,256]{2,1,0:T(8,128)(2,1)}, bf16[1024,256]{1,0:T(8,128)(2,1)}, f32[32,2304]{1,0:T(8,128)}, f32[48,768]{1,0:T(8,128)}, /*index=5*/f32[16,256]{1,0:T(8,128)}) custom-call(bf16[1024,768]{1,0:T(8,128)(2,1)} %get-tuple-element.52.proj, bf16[16,32,768]{2,1,0:T(8,128)(2,1)} %get-tuple-element.53.wq, ...), custom_call_target="tpu_custom_call" | custom-call | tf_op jit(solution)/shard_map/back/pallas_call | solution.py:1088
  117.6 8.9 %finish.1 = (bf16[8,512,1024]{2,1,0:T(8,128)(2,1)}, bf16[1024,256]{1,0:T(8,128)(2,1)}, bf16[1024,256]{1,0:T(8,128)(2,1)}, f32[32,768]{1,0:T(8,128)}, f32[768]{0:...) custom-call(bf16[8,512,1024]{2,1,0:T(8,128)(2,1)} %bitcast.12, ...), custom_call_target="tpu_custom_call" | custom-call | tf_op jit(solution)/shard_map/finish/pallas_call | solution.py:1199

commit v3 on v2

--- a/solution.py
+++ b/solution.py
@@ -78,9 +78,9 @@
 
 
 def middle_kernel(
-    dims, tok_ref, att_ref, og_ref, w_ref, vec_ref, raw_in,
-    out_ref, dh_ref, datt_ref, gw_ref, gvec_ref, raw_out,
-    act_s, slope_s, bounce, in_sem, out_sem,
+    dims, tok_ref, att_ref, og_ref, vec_ref, w_in, raw_in,
+    out_ref, dh_ref, datt_ref, gvec_ref, gw_out, raw_out,
+    act_s, slope_s, w_ref, gw_ref, bounce, w_sem, g_sem, in_sem, out_sem,
 ):
     cols, share, hw, fw = dims
     feat = vec_ref.shape[2]
@@ -90,6 +90,18 @@
     cut = min(512, fw)
     me = lax.axis_index("col")
 
+    total = w_ref.shape[3]
+    ranges = [(0, hw), (hw, fw), (hw + fw, fw)] if hw % 128 == 0 and fw % 128 == 0 else [(0, total)]
+
+    def columns(ref, n):
+        return ref.at[:, :, :, pl.ds(*ranges[n])]
+
+    loads = [pltpu.make_async_copy(columns(w_in, n), columns(w_ref, n), w_sem.at[n]) for n in range(len(ranges))]
+    stores = [pltpu.make_async_copy(columns(gw_ref, n), columns(gw_out, n), g_sem.at[n]) for n in range(len(ranges))]
+    split = len(ranges) == 3
+    for c in loads:
+        c.start()
+    loads[0].wait()
     takes = [pltpu.make_async_copy(raw_in.at[n], bounce.at[n], in_sem.at[n]) for n in range(slots)]
     puts = [pltpu.make_async_copy(bounce.at[n], raw_out.at[n], out_sem.at[n]) for n in range(slots)]
     for c in takes:
@@ -118,6 +130,9 @@
 
     chunks = [(c, o) for c in range(cols) for o in range(0, fw, cut)]
     hidden2 = normed1 + ff2_bias
+    if split:
+        loads[1].wait()
+        loads[2].wait()
     for c, o in chunks:
         at = c * fw + o
         bias = jnp.concatenate([vec_ref[c, 6 + (o + i) // feat : 7 + (o + i) // feat] for i in range(0, cut, feat)], axis=1)
@@ -154,6 +169,9 @@
         for i in range(0, cut, feat):
             gvec_ref[c, 6 + (o + i) // feat : 7 + (o + i) // feat] = sums[:, i : i + feat]
 
+    if split:
+        stores[1].start()
+        stores[2].start()
     rows[1] = col_sum(d_normed1 * xhat1)
     rows[2] = col_sum(d_normed1)
     d_hidden1 = norm_back(d_normed1 * gain1, xhat1, inv1)
@@ -172,7 +190,10 @@
             gvec_ref[c, i : i + 1] = rows[i][:, span]
         if spare:
             gvec_ref[c, 6 + fw // feat :] = jnp.zeros((spare, feat), F32)
+    stores[0].start()
     for c in puts:
+        c.wait()
+    for c in stores:
         c.wait()
 
 
@@ -182,7 +203,7 @@
     share = og.shape[1]
     hw = att.shape[1] * att.shape[3]
     fw = (w.shape[3] - hw) // 2
-    slots = 8
+    slots = 4
     pieces = (slots, raw.shape[0] * raw.shape[1] // slots, raw.shape[2])
     vmem = pl.BlockSpec(memory_space=pltpu.VMEM)
     anywhere = pl.BlockSpec(memory_space=pl.ANY)
@@ -192,22 +213,26 @@
             jax.ShapeDtypeStruct((cols, share, feat), BF16),
             jax.ShapeDtypeStruct((cols, share, feat), BF16),
             jax.ShapeDtypeStruct((cols, share, hw), BF16),
+            jax.ShapeDtypeStruct(vec.shape, F32),
             jax.ShapeDtypeStruct(w.shape, BF16),
-            jax.ShapeDtypeStruct(vec.shape, F32),
             jax.ShapeDtypeStruct(pieces, BF16),
         ],
-        in_specs=[vmem] * 5 + [anywhere],
-        out_specs=[vmem] * 5 + [anywhere],
+        in_specs=[vmem] * 4 + [anywhere] * 2,
+        out_specs=[vmem] * 4 + [anywhere] * 2,
         scratch_shapes=[
             pltpu.VMEM((share, cols * fw), BF16),
             pltpu.VMEM((share, cols * fw), F32),
+            pltpu.VMEM(w.shape, BF16),
+            pltpu.VMEM(w.shape, BF16),
             pltpu.VMEM(pieces, BF16),
+            pltpu.SemaphoreType.DMA((3,)),
+            pltpu.SemaphoreType.DMA((3,)),
             pltpu.SemaphoreType.DMA((slots,)),
             pltpu.SemaphoreType.DMA((slots,)),
         ],
         compiler_params=pltpu.CompilerParams(vmem_limit_bytes=60 << 20),
         name="middle",
-    )(tok, att, og, w, vec, raw.reshape(pieces))
+    )(tok, att, og, vec, w, raw.reshape(pieces))
     return *results[:-1], results[-1].reshape(raw.shape)
 
 
@@ -427,7 +452,7 @@
             if h == 1:
                 for p in range(len(pieces)):
                     f_own(0, p)
-            if h == 2:
+            if h == 3:
                 if cols == 2:
                     for j in offs:
                         x_got("wf", j).wait_recv()
@@ -453,7 +478,6 @@
             def _():
                 for j in offs:
                     x_got("tok2", j).wait_recv()
-                handle(0, 2)
 
             total = bias[...].reshape(1, -1).astype(F32)
             for c in range(cols):
@@ -463,7 +487,6 @@
             return carry
 
         lax.fori_loop(0, tok.shape[0] // chunk, project, 0)
-        handle(1, 2)
 
     @pl.when(pos == 0)
     def _():
@@ -517,7 +540,7 @@
     def _():
         att_send(step - 1)
 
-    at_step = {1: [(0, 3)], 2: [(1, 3)], 3: [(0, 4)], 5: [(1, 4)], 7: []}
+    at_step = {1: [(0, 2)], 2: [(1, 2)], 4: [(0, 3)], 5: [(1, 3)], 7: [(0, 4), (1, 4)]}
     for h in range(5, far + 1):
         at_step[7] += [(0, h), (1, h)]
     for n, todo in at_step.items():
@@ -907,13 +930,11 @@
 
     jobs = {
         0: [lambda: own_load().wait(), lambda: run_round(1)],
-        1: [v_second] + [lambda kind=kind, j=j: x_copy(kind, j).start() for kind in (1, 2) for j in offs],
-        2: [lambda: run_round(2, (0, 1))],
-        3: [lambda: run_round(2, (2,)), v_third],
-        4: [lambda: run_round(2, (3,)), lambda: run_round(3, (0,))],
-        5: [lambda: run_round(3, (1,))],
-        6: [lambda: run_round(3, (2, 3))],
-        7: [lambda: run_round(4, (0,))],
+        1: [v_second, *[lambda kind=kind, j=j: x_copy(kind, j).start() for kind in (1, 2) for j in offs]],
+        3: [v_third, lambda: run_round(2, (0,))],
+        4: [lambda: run_round(2, (1, 2))],
+        5: [lambda: run_round(2, (3,))],
+        7: [lambda: run_round(3, (0, 1))],
     }
 
     def spot(n):
@@ -983,7 +1004,8 @@
             x_copy(4, j).start()
         if pairs > 1:
             g_pair(last - 1).wait_send()
-        run_round(4, (1, 2, 3))
+        run_round(3, (2, 3))
+        run_round(4)
         g_weight(last)
         for t in range(5, far + 1):
             run_round(t)
@@ -1138,18 +1160,20 @@
     )(proj, wq, tok, datt, outp, dh, gvec, gw, prob, cot)
 
 
-def finish_kernel(cols, pg_in, out_in, ig_in, gw, gq, gv, pg, out, ig, wq, bq, wo, bo, n1g, n1s, w1, b1, w2, b2, n2g, n2s, bounce, in_sem, out_sem):
-    slots = bounce.shape[0]
-    takes = [pltpu.make_async_copy(pg_in.at[n], bounce.at[n], in_sem.at[n]) for n in range(slots)]
-    puts = [pltpu.make_async_copy(bounce.at[n], pg.at[n], out_sem.at[n]) for n in range(slots)]
+def finish_kernel(
+    pg_in, out_in, ig_in, gw, gq, gv, pg, out, ig, wq, bq, wo, bo, n1g, n1s, w1, b1, w2, b2, n2g, n2s,
+    bounce, out_s, ig_s, in_sem, out_sem,
+):
+    ways = [(pg_in.at[n], bounce.at[n], pg.at[n]) for n in range(bounce.shape[0])]
+    ways += [(out_in, out_s, out), (ig_in, ig_s, ig)]
+    slots = len(ways)
+    takes = [pltpu.make_async_copy(a, b, in_sem.at[n]) for n, (a, b, _) in enumerate(ways)]
+    puts = [pltpu.make_async_copy(b, c, out_sem.at[n]) for n, (_, b, c) in enumerate(ways)]
     for c in takes:
         c.start()
     shard = wq.shape[0]
     hw, fw = wo.shape[1], w1.shape[1]
-    feat = out.shape[1]
-    for c in range(cols):
-        out[c * out_in.shape[1] : (c + 1) * out_in.shape[1], :] = out_in[c]
-    ig[...] = ig_in[...]
+    feat = gv.shape[1]
     for n in range(slots // 2):
         takes[n].wait()
         puts[n].start()
@@ -1168,8 +1192,8 @@
         c.wait()
 
 
-def finish(cols, pg, out, ig, gw, gq, gv, hw, fw):
-    slots = 8
+def finish(pg, out, ig, gw, gq, gv, hw, fw):
+    slots = 4
     pieces = (slots, pg.shape[0] * pg.shape[1] // slots, pg.shape[2])
     total, feat = ig.shape
     shard = gw.shape[0]
@@ -1197,18 +1221,20 @@
         f32(feat),
     ]
     return pl.pallas_call(
-        functools.partial(finish_kernel, cols),
+        finish_kernel,
         out_shape=outs,
-        in_specs=[anywhere] + [vmem] * 5,
-        out_specs=[anywhere] + [vmem] * 14,
+        in_specs=[anywhere] * 3 + [vmem] * 3,
+        out_specs=[anywhere] * 3 + [vmem] * 12,
         scratch_shapes=[
             pltpu.VMEM(pieces, BF16),
-            pltpu.SemaphoreType.DMA((slots,)),
-            pltpu.SemaphoreType.DMA((slots,)),
+            pltpu.VMEM(ig.shape, BF16),
+            pltpu.VMEM(ig.shape, BF16),
+            pltpu.SemaphoreType.DMA((slots + 2,)),
+            pltpu.SemaphoreType.DMA((slots + 2,)),
         ],
         compiler_params=pltpu.CompilerParams(vmem_limit_bytes=60 << 20),
         name="finish",
-    )(pg.reshape(pieces), out, ig, gw, gq, gv)
+    )(pg.reshape(pieces), out.reshape(ig.shape), ig, gw, gq, gv)
 
 
 def per_device(
@@ -1243,13 +1269,13 @@
     raw, prob, tok_all, proj, wf_all, wq_all, vec_all, og_all, att_all = front(
         cols, rows_dev, seqs, head_count, tokens, qkv_weight, out_weight.T, ff1_weight, ff2_weight.T, sides, out_grad, qkv_bias, prev
     )
-    out, dh, datt, gw, gvec, raw = middle(tok_all, att_all, og_all, wf_all, vec_all, raw)
+    out, dh, datt, gvec, gw, raw = middle(tok_all, att_all, og_all, wf_all, vec_all, raw)
 
     prev_grad, output, input_grad, gw, gq, gv = back(
         cols, rows_dev, seqs, head_count, proj, wq_all, tok_all, datt, out, dh, gvec, gw, prob, cot
     )
     prev_grad, output, input_grad, *rest = finish(
-        cols, prev_grad, output, input_grad, gw, gq, gv, out_weight.shape[0], hidden
+        prev_grad, output, input_grad, gw, gq, gv, out_weight.shape[0], hidden
     )
     rest[2] = rest[2].T
     rest[8] = rest[8].T

time: 128 us -> 122 us (0.953)
  Pallas kernels: 126 us -> 121 us
    pallas_call x1, Pallas kernels: 50.1 us -> 45.5 us  [front(): pl.pallas_call(functools.partial(front_kernel, (cols, rows_dev, seqs, hea...]
where the time goes in v3:
time: 122 us
  Pallas kernels  121 us (99%)
    pallas_call x1, Pallas kernels, back(): pl.pallas_call(functools.partial(back_kernel, (cols, rows_dev, seqs, head...  50.4 us
    pallas_call x1, Pallas kernels, front(): pl.pallas_call(functools.partial(front_kernel, (cols, rows_dev, seqs, hea...  45.5 us
    pallas_call x1, Pallas kernels, middle(): pl.pallas_call(functools.partial(middle_kernel, (cols, share, hw, fw)), o...  15.9 us
    pallas_call x1, Pallas kernels, finish(): pl.pallas_call(finish_kernel, out_shape=outs, in_specs=[anywhere] * 3 + [...  9.16 us

profile of v3, /device:TPU:0, one launch (start us, length us, event | category | flops | bytes accessed | tf_op | source)
XLA Modules:
  0.0 121.8 jit_solution(13312458802980616983)
XLA Ops:
  0.7 45.5 %front.1 = (bf16[4,1024,1024]{2,1,0:T(8,128)(2,1)}, bf16[4,1024,1024]{2,1,0:T(8,128)(2,1)}, bf16[2,1024,256]{2,1,0:T(8,128)(2,1)}, bf16[1024,768]{1,0:T(8,128)(2...) custom-call(bf16[1024,256]{1,0:T(8,128)(2,1)} %tok.1, ...), custom_call_target="tpu_custom_call" | custom-call | tf_op jit(solution)/shard_map/front/pallas_call | solution.py:647
  46.1 15.9 %middle.1 = (bf16[2,512,256]{2,1,0:T(8,128)(2,1)}, bf16[2,512,256]{2,1,0:T(8,128)(2,1)}, bf16[2,512,256]{2,1,0:T(8,128)(2,1)}, f32[2,16,256]{2,1,0:T(8,128)}, bf...) custom-call(bf16[2,1024,256]{2,1,0:T(8,128)(2,1)} %get-tuple-element.54.tok_ref.tok, ...), custom_call_target="tpu_custom_call" | custom-call | tf_op jit(solution)/shard_map/middle/pallas_call | solution.py:210
  62.1 50.4 %back.1 = (bf16[4,1024,1024]{2,1,0:T(8,128)(2,1)}, bf16[2,512,256]{2,1,0:T(8,128)(2,1)}, bf16[1024,256]{1,0:T(8,128)(2,1)}, f32[32,2304]{1,0:T(8,128)}, f32[48,768]{1,0:T(8,128)}, /*index=5*/f32[16,256]{1,0:T(8,128)}) custom-call(bf16[1024,768]{1,0:T(8,128)(2,1)} %get-tuple-element.52.proj, bf16[16,32,768]{2,1,0:T(8,128)(2,1)} %get-tuple-element.53.wq, ...), custom_call_target="tpu_custom_call" | custom-call | tf_op jit(solution)/shard_map/back/pallas_call | solution.py:1110
  112.5 9.2 %finish.1 = (bf16[4,1024,1024]{2,1,0:T(8,128)(2,1)}, bf16[1024,256]{1,0:T(8,128)(2,1)}, bf16[1024,256]{1,0:T(8,128)(2,1)}, f32[32,768]{1,0:T(8,128)}, f32[768]{0...) custom-call(bf16[4,1024,1024]{2,1,0:T(8,128)(2,1)} %get-tuple-elemen, ...), custom_call_target="tpu_custom_call" | custom-call | tf_op jit(solution)/shard_map/finish/pallas_call | solution.py:1223

commit v4 on v3

--- a/solution.py
+++ b/solution.py
@@ -681,11 +681,11 @@
 
 
 def back_kernel(
-    dims, proj, wq, tok, datt, outp, dh, gvec, gw, prob, cot,
+    dims, proj, gvec, wq_in, tok_in, datt, outp, dh, gw, prob, cot,
     pg, out_all, ig, gwo, gqo, gvo,
     datt_s, out_s, dh_s, q_s, k_s, v_s, dq_s, dk_s, dv_s, dp_s,
     own_s, part_s, run_s, run_r, fin_s, fin_r,
-    gq_s, gq_p, gq_t, gq_r, ip_s, xi_s, xi_r, vp_s, vs_s, vx_s, vr_s,
+    gq_s, gq_p, gq_t, gq_r, ip_s, xi_s, xi_r, vp_s, vs_s, vx_s, vr_s, wq, tok,
     x_send, x_recv, p_send, p_recv, r_send, r_recv, g_send, g_recv, v_send, v_recv, l_sem,
 ):
     cols, rows_dev, seqs, heads, pairs, share, block = dims
@@ -724,6 +724,8 @@
     def to_chip(o):
         return (2 * chip_of(o) + core, me)
 
+    halves = [pl.ds(i * (total_rows // 2), total_rows // 2) for i in range(2)]
+
     def x_copy(kind, j):
         to = at.peer(j)
         src, dst = [
@@ -731,8 +733,9 @@
             lambda: (outp.at[to], out_s.at[me]),
             lambda: (dh.at[to], dh_s.at[me]),
             lambda: (fin_s.at[to], fin_r.at[me]),
-            lambda: (xi_s.at[j - 1], xi_r.at[j - 1]),
+            lambda: (xi_s.at[j - 1, halves[0]], xi_r.at[j - 1, halves[0]]),
             lambda: (vs_s.at[to], vx_s.at[me]),
+            lambda: (xi_s.at[j - 1, halves[1]], xi_r.at[j - 1, halves[1]]),
         ][kind]()
         return rcopy(src, dst, x_send.at[kind, j - 1], x_recv.at[kind, j - 1], at.col_peer(j))
 
@@ -743,8 +746,9 @@
             lambda: (outp.at[came], out_s.at[came]),
             lambda: (dh.at[came], dh_s.at[came]),
             lambda: (fin_s.at[came], fin_r.at[came]),
-            lambda: (xi_s.at[j - 1], xi_r.at[j - 1]),
+            lambda: (xi_s.at[j - 1, halves[0]], xi_r.at[j - 1, halves[0]]),
             lambda: (vs_s.at[came], vx_s.at[came]),
+            lambda: (xi_s.at[j - 1, halves[1]], xi_r.at[j - 1, halves[1]]),
         ][kind]()
         return rcopy(src, dst, x_send.at[kind, j - 1], x_recv.at[kind, j - 1], at.col_peer(j))
 
@@ -760,6 +764,12 @@
             pltpu.make_async_copy(datt.at[me], datt_s.at[me], l_sem.at[1]),
             pltpu.make_async_copy(outp.at[me], out_s.at[me], l_sem.at[2]),
             pltpu.make_async_copy(dh.at[me], dh_s.at[me], l_sem.at[3]),
+        ]
+
+    def late_loads():
+        return [
+            pltpu.make_async_copy(wq_in, wq, l_sem.at[4]),
+            pltpu.make_async_copy(tok_in, tok, l_sem.at[5]),
         ]
 
     def run_copy(k, p, way, t):
@@ -862,9 +872,10 @@
             value = value + gq_r[j, c].astype(F32)
         gqo[:, j * wide : (j + 1) * wide] = value
 
-    chunk = min(512, total_rows)
-
-    def input_part(j, n):
+    chunk = min(512, share)
+    parts_of_half = total_rows // 2 // chunk
+
+    def input_part(j, n, part=None):
         slots = rows_dev // cols
         w = wq[pl.ds(at.peer(n) * slots, slots), :, j * wide : (j + 1) * wide].reshape(slots * shard, wide)
 
@@ -881,7 +892,8 @@
                 ip_s[0, span, :] = value
             return carry
 
-        lax.fori_loop(0, total_rows // chunk, go, 0)
+        first = 0 if part is None else part * parts_of_half
+        lax.fori_loop(first, 2 * parts_of_half if part is None else first + parts_of_half, go, 0)
 
     @pl.when(step == 0)
     def _():
@@ -897,13 +909,17 @@
         order = [far] + [s * o for o in range(far - 1, 0, -1) for s in (1, -1)] + [0]
         for o in order:
             part_copy(o).start()
-        for c in locals_():
+        for c in locals_() + late_loads():
             c.start()
-        for c in locals_():
-            c.wait()
+        locals_()[0].wait()
         if seqs > 1:
             for j in offs:
                 x_got(0, j).wait_recv()
+
+    @pl.when(step == 1)
+    def _():
+        for c in locals_()[1:] + late_loads():
+            c.wait()
 
     if seqs == 1:
 
@@ -999,9 +1015,10 @@
     @pl.when(step == steps - 1)
     def _():
         last = pairs - 1
-        for j in offs:
-            input_part(last, j)
-            x_copy(4, j).start()
+        for part, kind in ((0, 4), (1, 6)):
+            for j in offs:
+                input_part(last, j, part)
+                x_copy(kind, j).start()
         if pairs > 1:
             g_pair(last - 1).wait_send()
         run_round(3, (2, 3))
@@ -1028,12 +1045,10 @@
         gvo[...] = value
         for j in range(pairs):
             g_last(j)
-        for j in offs:
-            x_got(4, j).wait_recv()
 
         def finish(i, carry):
-            c = i // (share // min(share, chunk))
-            rows = min(share, chunk)
+            rows = chunk
+            c = i // (share // rows)
             inner = pl.ds(pl.multiple_of(lax.rem(i, share // rows) * rows, rows), rows)
             span = pl.ds(pl.multiple_of(i * rows, rows), rows)
             value = ip_s[0, span, :] + dh_s[c, inner, :].astype(F32)
@@ -1042,14 +1057,17 @@
             ig[span, :] = value.astype(BF16)
             return carry
 
-        lax.fori_loop(0, total_rows // min(share, chunk), finish, 0)
+        for part, kind in ((0, 4), (1, 6)):
+            for j in offs:
+                x_got(kind, j).wait_recv()
+            lax.fori_loop(part * parts_of_half, (part + 1) * parts_of_half, finish, 0)
         value = fin_s[me].astype(F32)
         for j in offs:
             x_got(3, j).wait_recv()
             value = value + fin_r[at.peer(-j)].astype(F32)
         gwo[...] = value
         keep.wait()
-        for kind in range(6):
+        for kind in range(7):
             for j in offs:
                 x_copy(kind, j).wait_send()
         for o in range(chips):
@@ -1110,7 +1128,7 @@
     return pl.pallas_call(
         functools.partial(back_kernel, (cols, rows_dev, seqs, heads, pairs, share, block)),
         grid=(pairs * seqs * turns,),
-        in_specs=[whole(x.shape) for x in (proj, wq, tok, datt, outp, dh, gvec)] + [anywhere, blocks, blocks],
+        in_specs=[whole(proj.shape), whole(gvec.shape)] + [anywhere] * 6 + [blocks, blocks],
         out_specs=[blocks, anywhere] + [whole(o.shape) for o in outs[2:]],
         out_shape=outs,
         scratch_shapes=[
@@ -1141,8 +1159,10 @@
             pltpu.VMEM(gvec.shape, F32),
             pltpu.VMEM(gvec.shape, F32),
             pltpu.VMEM((chips,) + gvec.shape[1:], F32),
-            dma((6, cols - 1)),
-            dma((6, cols - 1)),
+            pltpu.VMEM(wq.shape, BF16),
+            pltpu.VMEM(tok.shape, BF16),
+            dma((7, cols - 1)),
+            dma((7, cols - 1)),
             dma((chips,)),
             dma((chips,)),
             dma((2, n, 2, far)),
@@ -1151,13 +1171,13 @@
             dma((pairs, chips)),
             dma((chips,)),
             dma((chips,)),
-            dma((4,)),
+            dma((6,)),
         ],
         compiler_params=pltpu.CompilerParams(
             collective_id=2, has_side_effects=True, vmem_limit_bytes=62 << 20
         ),
         name="back",
-    )(proj, wq, tok, datt, outp, dh, gvec, gw, prob, cot)
+    )(proj, gvec, wq, tok, datt, outp, dh, gw, prob, cot)
 
 
 def finish_kernel(

time: 122 us -> 122 us (level)
  no operation moved by 1% of the time
where the time goes in v4:
time: 122 us; the launch traced here: 121 us
  Pallas kernels  121 us (99%)
    pallas_call x1, Pallas kernels, back(): pl.pallas_call(functools.partial(back_kernel, (cols, rows_dev, seqs, head...  50 us
    pallas_call x1, Pallas kernels, front(): pl.pallas_call(functools.partial(front_kernel, (cols, rows_dev, seqs, hea...  45.5 us
    pallas_call x1, Pallas kernels, middle(): pl.pallas_call(functools.partial(middle_kernel, (cols, share, hw, fw)), o...  15.9 us
    pallas_call x1, Pallas kernels, finish(): pl.pallas_call(finish_kernel, out_shape=outs, in_specs=[anywhere] * 3 + [...  9.16 us

profile of v4, /device:TPU:0, one launch (start us, length us, event | category | flops | bytes accessed | tf_op | source)
XLA Modules:
  0.0 121.4 jit_solution(8341901067319263064)
XLA Ops:
  0.7 45.5 %front.1 = (bf16[4,1024,1024]{2,1,0:T(8,128)(2,1)}, bf16[4,1024,1024]{2,1,0:T(8,128)(2,1)}, bf16[2,1024,256]{2,1,0:T(8,128)(2,1)}, bf16[1024,768]{1,0:T(8,128)(2...) custom-call(bf16[1024,256]{1,0:T(8,128)(2,1)} %tok.1, ...), custom_call_target="tpu_custom_call" | custom-call | tf_op jit(solution)/shard_map/front/pallas_call | solution.py:647
  46.1 15.9 %middle.1 = (bf16[2,512,256]{2,1,0:T(8,128)(2,1)}, bf16[2,512,256]{2,1,0:T(8,128)(2,1)}, bf16[2,512,256]{2,1,0:T(8,128)(2,1)}, f32[2,16,256]{2,1,0:T(8,128)}, bf...) custom-call(bf16[2,1024,256]{2,1,0:T(8,128)(2,1)} %get-tuple-element.53.tok_ref.tok_in, ...), custom_call_target="tpu_custom_call" | custom-call | tf_op jit(solution)/shard_map/middle/pallas_call | solution.py:210
  62.1 50.0 %back.1 = (bf16[4,1024,1024]{2,1,0:T(8,128)(2,1)}, bf16[2,512,256]{2,1,0:T(8,128)(2,1)}, bf16[1024,256]{1,0:T(8,128)(2,1)}, f32[32,2304]{1,0:T(8,128)}, f32[48,768]{1,0:T(8,128)}, /*index=5*/f32[16,256]{1,0:T(8,128)}) custom-call(bf16[1024,768]{1,0:T(8,128)(2,1)} %get-tuple-element.52.proj, f32[2,16,256]{2,1,0:T(8,128)} %get-tuple-element.59.gvec, ...), custom_call_target="tpu_custom_call" | custom-call | tf_op jit(solution)/shard_map/back/pallas_call | solution.py:1128
  112.0 9.2 %finish.1 = (bf16[4,1024,1024]{2,1,0:T(8,128)(2,1)}, bf16[1024,256]{1,0:T(8,128)(2,1)}, bf16[1024,256]{1,0:T(8,128)(2,1)}, f32[32,768]{1,0:T(8,128)}, f32[768]{0...) custom-call(bf16[4,1024,1024]{2,1,0:T(8,128)(2,1)} %get-tuple-elemen, ...), custom_call_target="tpu_custom_call" | custom-call | tf_op jit(solution)/shard_map/finish/pallas_call | solution.py:1243
